TPU v7x, 256 devices: a whole 4x4x8 slice. The times are simulated.
256 devices in a mesh: rep: 1, dp: 256 (over x, y, z, core).
Axes of the slice: x: 4, y: 4, z: 8, core: 2. Of those that a mesh axis runs over, the one named last changes fastest.
Arguments:
- x: bfloat16 [256, 1024, 1024], P(('rep', 'dp'))
- dy: bfloat16 [256, 1024, 1024], P(('rep', 'dp'))
- w_gate: bfloat16 [2, 1024, 2816], replicated
- w_up: bfloat16 [2, 1024, 2816], replicated
- w_down: bfloat16 [2, 2816, 1024], replicated
- m_w_gate: float32 [2, 1024, 2816], replicated
- m_w_up: float32 [2, 1024, 2816], replicated
- m_w_down: float32 [2, 2816, 1024], replicated
- v_w_gate: float32 [2, 1024, 2816], replicated
- v_w_up: float32 [2, 1024, 2816], replicated
- v_w_down: float32 [2, 2816, 1024], replicated
Outputs:
- output 1: bfloat16 [2, 1024, 2816], P('rep')
- output 2: bfloat16 [2, 1024, 2816], P('rep')
- output 3: bfloat16 [2, 2816, 1024], P('rep')
- output 4: float32 [2, 1024, 2816], P('rep')
- output 5: float32 [2, 1024, 2816], P('rep')
- output 6: float32 [2, 2816, 1024], P('rep')
- output 7: float32 [2, 1024, 2816], P('rep')
- output 8: float32 [2, 1024, 2816], P('rep')
- output 9: float32 [2, 2816, 1024], P('rep')
All inputs are finite; a program needn't handle non-finite values.
Results may differ from a plain program's by a relative error of at most 0.022.
Values are sent between devices in bfloat16 or wider.
A program may use at most 768 MiB of HBM per device.

v0:
```python
import jax
import jax.numpy as jnp
from jax import lax
from jax.sharding import PartitionSpec as P

NAMES = ("w_gate", "w_up", "w_down")


def matmul(a, w):
    return jnp.dot(a, w, preferred_element_type=jnp.float32).astype(jnp.bfloat16)


def normed(h):
    wide = h.astype(jnp.float32)
    scale = lax.rsqrt(jnp.mean(wide**2, -1, keepdims=True) + 1e-6)
    return (wide * scale).astype(jnp.bfloat16)


def layer(h, w):
    a = normed(h)
    gate = jnp.dot(a, w["w_gate"], preferred_element_type=jnp.float32)
    up = jnp.dot(a, w["w_up"], preferred_element_type=jnp.float32)
    return h + matmul((jax.nn.silu(gate) * up).astype(jnp.bfloat16), w["w_down"])


def adamw(w, m, v, g):
    m = 0.9 * m + 0.1 * g
    v = 0.95 * v + 0.05 * g * g
    step = m * lax.rsqrt(v + 1e-8) + 0.1 * w
    return (w - 0.02 * step).astype(jnp.bfloat16), m, v


def solution(mesh):
    def step(x, dy, *arrays):
        weights, m, v = (arrays[i : i + 3] for i in (0, 3, 6))
        layers = weights[0].shape[0]
        h, kept = x[0], []
        for number in range(layers):
            kept.append(h)
            h = layer(h, {name: w[number] for name, w in zip(NAMES, weights, strict=True)})
        by_h, summed = dy[0], [None] * layers
        for number in reversed(range(layers)):
            _, back = jax.vjp(lambda w, h: layer(h, w), {name: w[number] for name, w in zip(NAMES, weights, strict=True)}, kept[number])
            by_w, by_h = back(by_h)
            summed[number] = [lax.psum(by_w[name], "dp") for name in NAMES]
        gradients = [jnp.stack([summed[number][i] for number in range(layers)]).astype(jnp.float32) for i in range(3)]
        new = [adamw(w.astype(jnp.float32), m, v, g) for w, m, v, g in zip(weights, m, v, gradients, strict=True)]
        return tuple(one[which] for which in range(3) for one in new)

    return jax.shard_map(
        step,
        mesh=mesh,
        in_specs=(P(("rep", "dp"), None, None),) * 2 + (P(None, None, None),) * 9,
        out_specs=(P("rep", None, None),) * 9,
        check_vma=False,
    )
```

profile of v0, /device:TPU:1, one launch (start us, length us, event | category | flops | bytes accessed | tf_op | source)
XLA Modules:
  0.0 756.1 jit_solution(11085353490233188341)
XLA Ops:
  7.2 0.0 all-reduce.3.cloned.1.call-start
  7.2 2.9 copy.20
  10.1 0.5 fusion.64
  10.6 0.9 copy-done.1
  11.4 4.1 copy.21
  15.5 11.1 %fusion.53 = bf16[1024,2816]{1,0:T(8,128)(2,1)} fusion(bf16[2,2816,1024]{2,1,0:T(8,128)(2,1)} %param.15, bf16[1,1024,1024]{2,1,0:T(8,128)(2,1)} %param.12), kind=kOutput, calls=%fused_computation.85 | convolution fusion | flops 5908463616 | bytes 13631488 | tf_op jit(solution)/shard_map/transpose(jvp())/dot_general | solution.py:10
  26.6 9.1 %fusion.44 = f32[1024,2816]{1,0:T(8,128)} fusion(bf16[2,1024,2816]{2,1,0:T(8,128)(2,1)S(1)} %bitcast.79, bf16[1,1024,1024]{2,1,0:T(8,128)(2,1)S(1)} %copy-done.5, f32[1024]{0:T(1024)S(1)} %add_rsqrt_fusion), kind=kOutput, calls=%fused_computation.72 | convolution fusion | flops 5908725760 | bytes 19402752 | tf_op jit(solution)/shard_map/dot_general | solution.py:21
  35.7 15.2 %multiply_convert_fusion.1 = (bf16[1024,2816]{1,0:T(8,128)(2,1)}, f32[1024,2816]{1,0:T(8,128)}) fusion(f32[1024,2816]{1,0:T(8,128)} %fusion.44, bf16[2,1024,2816]{2,1,0:T(8,128)(2,1)} %param.14, bf16[1,1024,1024]{2,1,0:T(8,128)(2,1)} %param.11, f32[1024]{0:T(1024)S(1)} %add_rsqrt_fusion), kind=kOutput, calls=%fused_computation.47 | convolution fusion | flops 5926027264 | bytes 36704256 | tf_op jit(solution)/shard_map/dot_general | solution.py:22
  51.0 10.4 %fusion.68 = (f32[1024]{0:T(1024)S(1)}, bf16[1024,1024]{0,1:T(8,128)(2,1)S(1)}) fusion(bf16[1024,2816]{1,0:T(8,128)(2,1)} %get-tuple-element.24, bf16[2,2816,1024]{2,1,0:T(8,128)(2,1)} %param.15, bf16[1,1024,1024]{1,2,0:T(8,128)(2,1)S(1)} %copy-done.2), kind=kOutput, calls=%fused_computation.99 | convolution fusion | flops 5910821888 | bytes 15732736 | tf_op jit(solution)/shard_map/dot_general | solution.py:10
  61.4 9.0 %fusion.29 = f32[1024,2816]{1,0:T(8,128)} fusion(bf16[2,1024,2816]{2,1,0:T(8,128)(2,1)S(1)} %bitcast.83, bf16[1024,1024]{0,1:T(8,128)(2,1)S(1)} %get-tuple-element.27, f32[1024]{0:T(1024)S(1)} %fusion.88), kind=kOutput, calls=%fused_computation.57 | convolution fusion | flops 5908725760 | bytes 19402752 | tf_op jit(solution)/shard_map/jvp()/dot_general | solution.py:22
  70.5 18.7 %fusion.17 = (bf16[1024,2816]{1,0:T(8,128)(2,1)}, f32[1024,2816]{1,0:T(8,128)}) fusion(f32[1024,2816]{1,0:T(8,128)} %fusion.29, bf16[1024,2816]{1,0:T(8,128)(2,1)} %fusion.53, bf16[2,1024,2816]{2,1,0:T(8,128)(2,1)} %param.13, bf16[1024,1024]{0,1:T(8,128)(2,1)S(1)} %get-tuple-element.27, f32[1024]{0:T(1024)S(1)} %fusion.88), kind=kOutput, calls=%fused_computation.35 | convolution fusion | flops 5943328768 | bytes 42471424 | tf_op jit(solution)/shard_map/jvp()/dot_general | solution.py:21
  89.2 13.0 %fusion.27 = bf16[1024,1024]{0,1:T(8,128)(2,1)} fusion(bf16[1024,2816]{1,0:T(8,128)(2,1)} %fusion.53, bf16[2,1024,2816]{2,1,0:T(8,128)(2,1)} %param.14, f32[1024,2816]{1,0:T(8,128)} %get-tuple-element.29), kind=kOutput, calls=%fused_computation.51 | convolution fusion | flops 5922881536 | bytes 25165824 | tf_op jit(solution)/shard_map/transpose(jvp())/dot_general | solution.py:22
  102.2 12.4 %convert_bitcast_fusion.2 = bf16[1,1024,2816]{2,1,0:T(8,128)(2,1)} fusion(bf16[1024,2816]{1,0:T(8,128)(2,1)} %fusion.53, bf16[1024,1024]{0,1:T(8,128)(2,1)S(1)} %get-tuple-element.27, f32[1024]{0:T(1024)S(1)} %fusion.88, f32[1024,2816]{1,0:T(8,128)} %get-tuple-element.29), kind=kOutput, calls=%fused_computation.76 | convolution fusion | flops 5928910848 | bytes 25169920 | tf_op jit(solution)/shard_map/transpose(jvp())/dot_general | solution.py:22
  114.5 12.9 %convert_bitcast_fusion = bf16[1,2816,1024]{2,1,0:T(8,128)(2,1)} fusion(f32[1024,2816]{1,0:T(8,128)} %fusion.29, bf16[1,1024,1024]{2,1,0:T(8,128)(2,1)S(1)} %copy-done.6, f32[1024,2816]{1,0:T(8,128)} %get-tuple-element.29), kind=kOutput, calls=%fused_computation.74 | convolution fusion | flops 5925765120 | bytes 30932992 | tf_op jit(solution)/shard_map/transpose(jvp())/dot_general | solution.py:10
  127.4 11.2 %convert_bitcast_fusion.4 = bf16[1,1024,2816]{2,1,0:T(8,128)(2,1)} fusion(bf16[1024,2816]{1,0:T(8,128)(2,1)} %get-tuple-element.28, bf16[1024,1024]{0,1:T(8,128)(2,1)S(1)} %get-tuple-element.27, f32[1024]{0:T(1024)S(1)} %fusion.88), kind=kOutput, calls=%fused_computation.78 | convolution fusion | flops 5908725760 | bytes 13635584 | tf_op jit(solution)/shard_map/transpose(jvp())/dot_general | solution.py:21
  138.6 8.6 %fusion.70 = (f32[1024]{0:T(1024)S(1)}, bf16[1024,1024]{0,1:T(8,128)(2,1)S(1)}) fusion(bf16[1024,1024]{0,1:T(8,128)(2,1)S(1)} %get-tuple-element.27, bf16[1024,1024]{0,1:T(8,128)(2,1)S(1)} %copy-done.10, bf16[1024,2816]{1,0:T(8,128)(2,1)} %get-tuple-element.28, bf16[2,1024,2816]{2,1,0:T(8,128)(2,1)S(1)} %bitcast.81), kind=kOutput, calls=%fused_computation.101 | convolution fusion | flops 5910821888 | bytes 17829888 | tf_op jit(solution)/shard_map/transpose(jvp())/dot_general | solution.py:21
  147.3 1.6 fusion.72
  148.8 9.2 %fusion.50 = bf16[1024,2816]{1,0:T(8,128)(2,1)S(1)} fusion(bf16[1024,1024]{0,1:T(8,128)(2,1)S(1)} %fusion.72, bf16[2,2816,1024]{2,1,0:T(8,128)(2,1)} %param.15), kind=kOutput, calls=%fused_computation.84 | convolution fusion | flops 5908463616 | bytes 13631488 | tf_op jit(solution)/shard_map/transpose(jvp())/dot_general | solution.py:10
  158.0 13.1 %convert_bitcast_fusion.1 = bf16[1,2816,1024]{2,1,0:T(8,128)(2,1)} fusion(bf16[1024,2816]{1,0:T(8,128)(2,1)} %get-tuple-element.24, bf16[1024,1024]{0,1:T(8,128)(2,1)S(1)} %fusion.72), kind=kOutput, calls=%fused_computation.75 | convolution fusion | flops 5908463616 | bytes 13631488 | tf_op jit(solution)/shard_map/transpose(jvp())/dot_general | solution.py:10
  171.1 11.4 %convert_bitcast_fusion.3 = bf16[1,1024,2816]{2,1,0:T(8,128)(2,1)} fusion(bf16[1024,2816]{1,0:T(8,128)(2,1)S(1)} %fusion.50, f32[1024,2816]{1,0:T(8,128)} %fusion.44, bf16[1,1024,1024]{1,2,0:T(8,128)(2,1)S(1)} %copy-done.3, f32[1024]{0:T(1024)S(1)} %copy-done.8), kind=kOutput, calls=%fused_computation.77 | convolution fusion | flops 5928910848 | bytes 25169920 | tf_op jit(solution)/shard_map/transpose(jvp())/dot_general | solution.py:22
  182.5 14.6 %convert_bitcast_fusion.5 = bf16[1,1024,2816]{2,1,0:T(8,128)(2,1)} fusion(f32[1024,2816]{1,0:T(8,128)} %fusion.44, f32[1024,2816]{1,0:T(8,128)} %get-tuple-element.25, bf16[1024,2816]{1,0:T(8,128)(2,1)} %copy-done.9, bf16[1,1024,1024]{1,2,0:T(8,128)(2,1)S(1)} %copy-done.3, f32[1024]{0:T(1024)S(1)} %copy-done.8), kind=kOutput, calls=%fused_computation.79 | convolution fusion | flops 5943328768 | bytes 36704256 | tf_op jit(solution)/shard_map/transpose(jvp())/dot_general | solution.py:21
  197.1 428.4 %all-reduce.3.cloned.1.call-done = (bf16[1,1024,2816]{2,1,0:T(8,128)(2,1)}, bf16[1,1024,2816]{2,1,0:T(8,128)(2,1)}, bf16[1,1024,2816]{2,1,0:T(8,128)(2,1)}, bf16...) async-done(((bf16[1,1024,2816]{2,1,0:T(8,128)(2,1)}, bf16[1,1024,2816]{2,1,0:T(8,128)(2,1)}, ...) | async-done | bytes 34603024 | tf_op jit(solution)/shard_map/psum | solution.py:45
  625.5 40.9 %fusion.10 = (bf16[2,2816,1024]{2,1,0:T(8,128)(2,1)}, f32[2,2816,1024]{2,1,0:T(8,128)}, f32[2,2816,1024]{2,1,0:T(8,128)}) fusion(bf16[2,2816,1024]{2,1,0:T(8,128)(2,1)} %param.15, bf16[1,2816,1024]{2,1,0:T(8,128)(2,1)} %get-tuple-element.13, bf16[1,2816,1024]{2,1,0:T(8,128)(2,1)} %get-tuple-element.14, f32[2,2816,1024]{2,1,0:T(8,128)} %param.21, ...), kind=kLoop, calls=%fused_computation.22 | loop fusion | flops 109576192 | bytes 126877696 | tf_op jit(solution)/shard_map/convert_element_type | solution.py:30
  666.4 82.7 %fusion.2 = (bf16[2,1024,2816]{2,1,0:T(8,128)(2,1)}, f32[2,1024,2816]{2,1,0:T(8,128)}, f32[2,1024,2816]{2,1,0:T(8,128)}, bf16[2,1024,2816]{2,1,0:T(8,128)(2,1)},...) fusion(bf16[2,1024,2816]{2,1,0:T(8,128)(2,1)} %param.13, bf16[1,1024,2816]{2,1,0:T(8,128)(2,1)S(1)} %copy-done.4, ...), kind=kLoop, calls=%fused_computation.14 | loop fusion | flops 219152384 | bytes 253755392 | tf_op jit(solution)/shard_map/convert_element_type | solution.py:30
  (46 shorter events, 0.1 us)
Async XLA Ops:
  7.2 618.3 %all-reduce.3.cloned.1.call-start = ((), (), s32[]{:S(2)}) async-start(), calls=%async_computation | async-start | bytes 69206016 | tf_op jit(solution)/shard_map/psum | solution.py:45
  10.1 1.3 copy-start.1
  11.4 24.3 %copy-start.7 = (f32[1024]{0:T(1024)}, f32[1024]{0:T(1024)S(1)}, u32[]{:S(2)}) copy-start(f32[1024]{0:T(1024)S(1)} %add_rsqrt_fusion) | copy-start | bytes 12292
  11.4 15.2 %slice-start = ((s8[11534336]{0:T(1024)(128)(4,1)}), s8[3145728]{0:T(1024)(128)(4,1)S(1)}, s32[]{:S(2)}) async-start(s8[11534336]{0:T(1024)(128)(4,1)} %bitcast.78), calls=%async_computation.1 | async-start | bytes 6291456
  15.5 11.1 %slice-start.1 = ((s8[11534336]{0:T(1024)(128)(4,1)}), s8[4194304]{0:T(1024)(128)(4,1)S(1)}, s32[]{:S(2)}) async-start(s8[11534336]{0:T(1024)(128)(4,1)} %bitcast.78), calls=%async_computation.2 | async-start | bytes 8388608
  15.5 11.1 %slice-start.2 = ((s8[11534336]{0:T(1024)(128)(4,1)}), s8[4194304]{0:T(1024)(128)(4,1)S(1)}, s32[]{:S(2)}) async-start(s8[11534336]{0:T(1024)(128)(4,1)} %bitcast.78), calls=%async_computation.3 | async-start | bytes 8388608
  15.5 11.1 %copy-start.5 = (bf16[1,1024,1024]{2,1,0:T(8,128)(2,1)S(1)}, bf16[1,1024,1024]{2,1,0:T(8,128)(2,1)}, u32[]{:S(2)}) copy-start(bf16[1,1024,1024]{2,1,0:T(8,128)(2,1)} %param.11) | copy-start | bytes 6291460
  35.7 15.2 %copy-start.2 = (bf16[1,1024,1024]{1,2,0:T(8,128)(2,1)S(1)}, bf16[1,1024,1024]{1,2,0:T(8,128)(2,1)}, u32[]{:S(2)}) copy-start(bf16[1,1024,1024]{1,2,0:T(8,128)(2,1)} %copy-done.1) | copy-start | bytes 6291460
  35.7 25.7 %slice-start.6 = ((s8[11534336]{0:T(1024)(128)(4,1)}), s8[3145728]{0:T(1024)(128)(4,1)S(1)}, s32[]{:S(2)}) async-start(s8[11534336]{0:T(1024)(128)(4,1)} %bitcast.82), calls=%async_computation.7 | async-start | bytes 6291456
  35.7 25.7 %slice-start.7 = ((s8[11534336]{0:T(1024)(128)(4,1)}), s8[4194304]{0:T(1024)(128)(4,1)S(1)}, s32[]{:S(2)}) async-start(s8[11534336]{0:T(1024)(128)(4,1)} %bitcast.82), calls=%async_computation.8 | async-start | bytes 8388608
  51.0 10.5 %slice-start.8 = ((s8[11534336]{0:T(1024)(128)(4,1)}), s8[4194304]{0:T(1024)(128)(4,1)S(1)}, s32[]{:S(2)}) async-start(s8[11534336]{0:T(1024)(128)(4,1)} %bitcast.82), calls=%async_computation.9 | async-start | bytes 8388608
  102.2 12.4 %copy-start.6 = (bf16[1,1024,1024]{2,1,0:T(8,128)(2,1)S(1)}, bf16[1,1024,1024]{2,1,0:T(8,128)(2,1)}, u32[]{:S(2)}) copy-start(bf16[1,1024,1024]{2,1,0:T(8,128)(2,1)} %param.12) | copy-start | bytes 6291460
  102.2 36.4 %slice-start.3 = ((s8[11534336]{0:T(1024)(128)(4,1)}), s8[4194304]{0:T(1024)(128)(4,1)S(1)}, s32[]{:S(2)}) async-start(s8[11534336]{0:T(1024)(128)(4,1)} %bitcast.80), calls=%async_computation.4 | async-start | bytes 8388608
  102.2 36.4 %slice-start.4 = ((s8[11534336]{0:T(1024)(128)(4,1)}), s8[4194304]{0:T(1024)(128)(4,1)S(1)}, s32[]{:S(2)}) async-start(s8[11534336]{0:T(1024)(128)(4,1)} %bitcast.80), calls=%async_computation.5 | async-start | bytes 8388608
  114.5 24.1 %slice-start.5 = ((s8[11534336]{0:T(1024)(128)(4,1)}), s8[3145728]{0:T(1024)(128)(4,1)S(1)}, s32[]{:S(2)}) async-start(s8[11534336]{0:T(1024)(128)(4,1)} %bitcast.80), calls=%async_computation.6 | async-start | bytes 6291456
  127.4 11.2 %copy-start.10 = (bf16[1024,1024]{0,1:T(8,128)(2,1)S(1)}, bf16[1024,1024]{0,1:T(8,128)(2,1)}, u32[]{:S(2)}) copy-start(bf16[1024,1024]{0,1:T(8,128)(2,1)} %fusion.27) | copy-start | bytes 6291460
  138.6 8.6 %copy-start = (bf16[1,1024,1024]{1,2,0:T(8,128)(2,1)S(1)}, bf16[1,1024,1024]{1,2,0:T(8,128)(2,1)}, u32[]{:S(2)}) copy-start(bf16[1,1024,1024]{1,2,0:T(8,128)(2,1)} %copy.21) | copy-start | bytes 6291460
  158.0 13.1 %copy-start.9 = (bf16[1024,2816]{1,0:T(8,128)(2,1)}, bf16[1024,2816]{1,0:T(8,128)(2,1)S(1)}, u32[]{:S(2)}) copy-start(bf16[1024,2816]{1,0:T(8,128)(2,1)S(1)} %fusion.50) | copy-start | bytes 17301508
  158.0 13.1 %copy-start.3 = (bf16[1,1024,1024]{1,2,0:T(8,128)(2,1)S(1)}, bf16[1,1024,1024]{1,2,0:T(8,128)(2,1)}, u32[]{:S(2)}) copy-start(bf16[1,1024,1024]{1,2,0:T(8,128)(2,1)} %copy-done.1) | copy-start | bytes 6291460
  158.0 13.1 %copy-start.8 = (f32[1024]{0:T(1024)S(1)}, f32[1024]{0:T(1024)}, u32[]{:S(2)}) copy-start(f32[1024]{0:T(1024)} %copy-done.7) | copy-start | bytes 12292
  625.5 40.9 %copy-start.4 = (bf16[1,1024,2816]{2,1,0:T(8,128)(2,1)S(1)}, bf16[1,1024,2816]{2,1,0:T(8,128)(2,1)}, u32[]{:S(2)}) copy-start(bf16[1,1024,2816]{2,1,0:T(8,128)(2,1)} %get-tuple-element.9) | copy-start | bytes 17301508
Sparse Core Ops, SparseCore 0:
  197.2 428.2 all-reduce.2
where the time goes:
time: 764 us; the launch traced here: 756 us
  waiting for transfers between devices  428 us (56%)
  matrix products  180 us (24%)
  other arithmetic  126 us (16%)
  between operations  14.5 us (2%)
  local copies, waits for them, and re-layouts  7.88 us (1%)
    psum x1, waiting for transfers between devices, step(): summed[number] = [lax.psum(by_w[name], 'dp') for name in NAMES]  428 us
    convert_element_type x2, other arithmetic, adamw(): return ((w - 0.02 * step).astype(jnp.bfloat16), m, v)  124 us
    dot_general x5, matrix products, layer(): gate = jnp.dot(a, w['w_gate'], preferred_element_type=jnp.float32)  62.1 us
    dot_general x5, matrix products, layer(): up = jnp.dot(a, w['w_up'], preferred_element_type=jnp.float32)  61 us
    dot_general x5, matrix products, matmul(): jnp.dot(a, w, preferred_element_type=jnp.float32).astype(jnp.bfloat16)  56.6 us
  transfers between devices with their start and end apart: 1, of which 1 were waited for; matrix products, arithmetic and copies ran while one was open for 0% of the time, Pallas kernels for 0%

commit v1 on v0

v1 whole, which is shorter than its diff:
```python
import functools

import jax
import jax.numpy as jnp
from jax import lax
from jax.experimental import pallas as pl
from jax.experimental.pallas import tpu as pltpu
from jax.sharding import PartitionSpec as P

MESH = pl.DeviceIdType.MESH

SIZE = {"x": 4, "y": 4, "z": 8}
TILES = 2816
HALF = TILES // 2
COLORS = []
_start = 0
for _axes, _unit, _first in (("xyz", 4, 2), ("yxz", 4, 2), ("zxy", 3, 0)):
    _n3 = _unit
    _n2 = _n3 * SIZE[_axes[2]]
    _n1 = _n2 * SIZE[_axes[1]]
    COLORS.append((_axes, _start, (_n1, _n2, _n3), _first))
    _start += _n1 * SIZE[_axes[0]]
assert _start == HALF
MATRICES = 6
BATCH = 3
LAG = 3


def ring_slots(n, hops):
    slots, at = [], 0
    for hop in range(hops):
        row = []
        for way in range(2):
            first = n - n // 2 if way == 0 else n // 2
            size = first if hop == 0 else n
            row.append((at, size))
            at += size
        slots.append(row)
    return slots, at


class Layout:
    def __init__(self):
        self.r1, self.r2, self.r3, self.s3, self.fin = [], [], [], [], []
        a1 = a2 = a3 = s3 = fin = 0
        self.sem = {}
        for c, (axes, _, (n1, n2, n3), _) in enumerate(COLORS):
            h1, h2, k3 = SIZE[axes[0]] // 2, SIZE[axes[1]] // 2, SIZE[axes[2]]
            slots, size = ring_slots(n1, h1)
            self.r1.append([[(a1 + s, n) for s, n in row] for row in slots])
            a1 += size
            slots, size = ring_slots(n2, h2)
            self.r2.append([[(a2 + s, n) for s, n in row] for row in slots])
            a2 += size
            self.r3.append(a3)
            a3 += (k3 - 1) * n3
            self.s3.append(s3)
            s3 += n2
            self.fin.append(fin)
            fin += n3
            for kind, count in (("r1", 2 * h1), ("r2", 2 * h2), ("r3", 1), ("g3", 1), ("g2", 2 * h2), ("g1", 2 * h1)):
                self.sem[c, kind] = len(self.sem_list) if hasattr(self, "sem_list") else 0
                if not hasattr(self, "sem_list"):
                    self.sem_list = []
                self.sem[c, kind] = len(self.sem_list)
                self.sem_list += [kind] * count
        self.n1, self.n2, self.n3, self.ns, self.nf = a1, a2, a3, s3, fin
        self.sems = len(self.sem_list)


LAY = Layout()


def out_index(m):
    return m % BATCH * 2 + (1 - m // BATCH)


def add_tiles(dst, dst_at, size, terms, chunk=8):
    def some(at, n):
        total = None
        for ref, start in terms:
            value = ref[pl.ds(start + at, n)].astype(jnp.float32)
            total = value if total is None else total + value
        dst[pl.ds(dst_at + at, n)] = total.astype(jnp.bfloat16)

    full = size // chunk
    if full > 1:
        lax.fori_loop(0, full, lambda i, _: (some(i * chunk, chunk), 0)[1], 0)
    elif full == 1:
        some(0, chunk)
    if size % chunk:
        some(full * chunk, size % chunk)


def reduce_kernel(*refs):
    grads, (out, own, par, r1, r2, r3, s3, fin, send_rs, send_ag, recv, pair, load) = refs[:MATRICES], refs[MATRICES:]
    me = lax.axis_index("dp")
    core = me % 2
    place = {"x": me // 64, "y": me // 16 % 4, "z": me // 2 % 8}

    def device(axis=None, by=0):
        at = dict(place)
        c = core
        if axis is None:
            c = 1 - core
        else:
            at[axis] = (at[axis] + by) % SIZE[axis]
        return (0, ((at["x"] * 4 + at["y"]) * 8 + at["z"]) * 2 + c)

    barrier = pltpu.get_barrier_semaphore()
    peers = [device()] + [device("x", 1), device("x", -1)] + [device("y", d) for d in (1, 2, 3)] + [device("z", d) for d in range(1, 8)]
    for peer in peers:
        pl.semaphore_signal(barrier, inc=1, device_id=peer, device_id_type=MESH)

    mine, theirs = core * HALF, (1 - core) * HALF

    def remote(src, dst, send, receive, to):
        return pltpu.make_async_remote_copy(
            src_ref=src, dst_ref=dst, send_sem=send, recv_sem=receive, device_id=to, device_id_type=MESH
        )

    def arrived(ref, n, sem):
        pltpu.make_async_copy(ref.at[pl.ds(0, n)], ref.at[pl.ds(0, n)], sem).wait()

    for m in range(MATRICES):
        pltpu.make_async_copy(grads[m].at[pl.ds(mine, HALF)], own.at[m], load.at[m, 0]).start()
    pl.semaphore_wait(barrier, len(peers))
    for m in range(MATRICES):
        remote(grads[m].at[pl.ds(theirs, HALF)], par.at[m], send_rs.at[m], pair.at[m, 0], device()).start()

    def sem(m, c, kind, i=0):
        return recv.at[m, LAY.sem[c, kind] + i]

    def color_stage(c, stage, m):
        axes, start, (n1, n2, n3), _ = COLORS[c]
        k1, k2, k3 = (SIZE[a] for a in axes)
        p1, p2, p3 = (place[a] for a in axes)
        h1, h2 = k1 // 2, k2 // 2
        o, q, a1, a2, a3 = own.at[m], par.at[m], r1.at[m], r2.at[m], r3.at[m]
        result = out.at[out_index(m)]
        base2 = start + p1 * n1
        base3 = base2 + p2 * n2
        shard = base3 + p3 * n3

        def ring_reduce(axis, k, p, n, base, hop, slots, arrivals, kind, more):
            h = k // 2
            j = h - hop
            for way, sign in ((0, 1), (1, -1)):
                owner = (p + sign * j) % k
                at = base + owner * n
                lo, size = (0, n) if j < h else ((0, n - n // 2) if way == 0 else (n - n // 2, n // 2))
                extra = [(ref, where + owner * n) for ref, where in more]
                if hop == 0:
                    add_tiles(o, at + lo, size, [(o, at + lo), (q, at + lo)] + [(r, w + lo) for r, w in extra])
                else:
                    there, got = slots[hop - 1][way]
                    arrived(arrivals, got, sem(m, c, kind, 2 * (hop - 1) + way))
                    if got == n:
                        add_tiles(o, at, n, [(o, at), (q, at)] + extra + [(arrivals, there)])
                    else:
                        first = 0 if way == 0 else n - got
                        add_tiles(o, at + first, got, [(o, at + first), (q, at + first)] + [(r, w + first) for r, w in extra] + [(arrivals, there)])
                        other, rest = (got, n - got) if way == 0 else (0, n - got)
                        add_tiles(o, at + other, rest, [(o, at + other), (q, at + other)] + [(r, w + other) for r, w in extra])
                there, size2 = slots[hop][way]
                assert size2 == size
                remote(
                    o.at[pl.ds(at + lo, size)], arrivals.at[pl.ds(there, size)], send_rs.at[m], sem(m, c, kind, 2 * hop + way), device(axis, sign)
                ).start()

        def ring_wait(k, slots, arrivals, kind):
            h = k // 2
            for way in range(2):
                arrived(arrivals, slots[h - 1][way][1], sem(m, c, kind, 2 * (h - 1) + way))

        def gather_sizes(k, n, hop):
            h = k // 2
            return [(0, n), (0, n)] if hop < h - 1 else [(0, n - n // 2), (n - n // 2, n // 2)]

        def gather_wait(k, n, hop, kind):
            for way in range(2):
                arrived(result, gather_sizes(k, n, hop)[way][1], sem(m, c, kind, 2 * hop + way))

        def ring_gather(axis, k, p, n, base, hop, kind):
            if hop:
                gather_wait(k, n, hop - 1, kind)
            for way, sign in ((0, 1), (1, -1)):
                lo, size = gather_sizes(k, n, hop)[way]
                at = mine + base + (p - sign * hop) % k * n + lo
                piece = result.at[pl.ds(at, size)]
                remote(piece, piece, send_ag.at[m], sem(m, c, kind, 2 * hop + way), device(axis, sign)).start()

        last1 = [(a1, LAY.r1[c][h1 - 1][way][0]) for way in range(2)]
        last2 = [(a2, LAY.r2[c][h2 - 1][way][0]) for way in range(2)]
        if stage < h1:
            ring_reduce(axes[0], k1, p1, n1, start, stage, LAY.r1[c], a1, "r1", [])
            return
        stage -= h1
        if stage < h2:
            if stage == 0:
                ring_wait(k1, LAY.r1[c], a1, "r1")
            ring_reduce(axes[1], k2, p2, n2, base2, stage, LAY.r2[c], a2, "r2", last1)
            return
        stage -= h2
        if stage == 0:
            ring_wait(k2, LAY.r2[c], a2, "r2")
            add_tiles(s3.at[m], LAY.s3[c], n2, [(o, base3), (q, base3)] + [(r, w + p2 * n2) for r, w in last1] + last2)
            for d in range(1, k3):
                owner = (p3 + d) % k3
                remote(
                    s3.at[m, pl.ds(LAY.s3[c] + owner * n3, n3)],
                    a3.at[pl.ds(LAY.r3[c] + (d - 1) * n3, n3)],
                    send_rs.at[m],
                    sem(m, c, "r3"),
                    device(axes[2], d),
                ).start()
            return
        stage -= 1
        if stage == 0:
            arrived(a3, (k3 - 1) * n3, sem(m, c, "r3"))
            terms = [(o, shard), (q, shard)] + [(r, w + p2 * n2 + p3 * n3) for r, w in last1] + [(r, w + p3 * n3) for r, w in last2]
            terms += [(a3, LAY.r3[c] + (d - 1) * n3) for d in range(1, k3)]
            add_tiles(fin.at[m], LAY.fin[c], n3, terms)
            piece = fin.at[m, pl.ds(LAY.fin[c], n3)]
            place_of = result.at[pl.ds(mine + shard, n3)]
            pltpu.make_async_copy(piece, place_of, load.at[m, 1 + c]).start()
            for d in range(1, k3):
                remote(piece, place_of, send_ag.at[m], sem(m, c, "g3"), device(axes[2], d)).start()
            return
        stage -= 1
        if stage < h2:
            if stage == 0:
                arrived(result, n3, load.at[m, 1 + c])
                arrived(result, (k3 - 1) * n3, sem(m, c, "g3"))
            ring_gather(axes[1], k2, p2, n2, base2, stage, "g2")
            return
        stage -= h2
        if stage < h1:
            if stage == 0:
                gather_wait(k2, n2, h2 - 1, "g2")
            ring_gather(axes[0], k1, p1, n1, start, stage, "g1")
            return
        stage -= h1
        if stage == 0:
            gather_wait(k1, n1, h1 - 1, "g1")

    def stages_of(c):
        axes = COLORS[c][0]
        return 2 * (SIZE[axes[0]] // 2 + SIZE[axes[1]] // 2) + 3

    ends = max(COLORS[c][3] + stages_of(c) for c in range(3))

    def slot(s, m):
        result = out.at[out_index(m)]
        if s == 0:
            arrived(own.at[m], HALF, load.at[m, 0])
            arrived(par.at[m], HALF, pair.at[m, 0])
        for c in (2, 0, 1):
            i = s - COLORS[c][3]
            if 0 <= i < stages_of(c):
                color_stage(c, i, m)
        if s == ends:
            half = result.at[pl.ds(mine, HALF)]
            remote(half, half, send_ag.at[m], pair.at[m, 1], device()).start()

    for s in range(ends + 1 + LAG):
        for batch in range(2):
            i = s - batch * LAG
            if 0 <= i <= ends:
                lax.fori_loop(batch * BATCH, (batch + 1) * BATCH, lambda m, _: (slot(i, m), 0)[1], 0)

    sent = HALF + LAY.n1 + LAY.n2 + LAY.n3

    def finish(m, _):
        result = out.at[out_index(m)]
        arrived(result, HALF, pair.at[m, 1])
        arrived(result, sent, send_rs.at[m])
        arrived(result, sent, send_ag.at[m])
        return 0

    lax.fori_loop(0, MATRICES, finish, 0)


def reduce_gradients(grads):
    tiles = lambda *n: pltpu.VMEM((MATRICES, *n, 8, 128), jnp.bfloat16)
    dma = pltpu.SemaphoreType.DMA
    return pl.pallas_call(
        reduce_kernel,
        out_shape=jax.ShapeDtypeStruct((MATRICES, TILES, 8, 128), jnp.bfloat16),
        in_specs=[pl.BlockSpec(memory_space=pl.ANY)] * MATRICES,
        out_specs=pl.BlockSpec(memory_space=pl.ANY),
        scratch_shapes=[
            tiles(HALF), tiles(HALF), tiles(LAY.n1), tiles(LAY.n2), tiles(LAY.n3), tiles(LAY.ns), tiles(LAY.nf),
            dma((MATRICES,)), dma((MATRICES,)), dma((MATRICES, LAY.sems)), dma((MATRICES, 2)), dma((MATRICES, 4)),
        ],
        compiler_params=pltpu.CompilerParams(collective_id=0, has_side_effects=True, vmem_limit_bytes=58 * 2**20),
        name="reduce_gradients",
    )(*grads)


NAMES = ("w_gate", "w_up", "w_down")

def matmul(a, w):
    return jnp.dot(a, w, preferred_element_type=jnp.float32).astype(jnp.bfloat16)


def normed(h):
    wide = h.astype(jnp.float32)
    scale = lax.rsqrt(jnp.mean(wide**2, -1, keepdims=True) + 1e-6)
    return (wide * scale).astype(jnp.bfloat16)


def layer(h, w):
    a = normed(h)
    gate = jnp.dot(a, w["w_gate"], preferred_element_type=jnp.float32)
    up = jnp.dot(a, w["w_up"], preferred_element_type=jnp.float32)
    return h + matmul((jax.nn.silu(gate) * up).astype(jnp.bfloat16), w["w_down"])


def adamw_kernel(w, m, v, g, new_w, new_m, new_v):
    g = g[0].astype(jnp.float32)
    m = 0.9 * m[...] + 0.1 * g
    v = 0.95 * v[...] + 0.05 * g * g
    w = w[...].astype(jnp.float32)
    step = m * lax.rsqrt(v + 1e-8) + 0.1 * w
    new_w[...] = (w - 0.02 * step).astype(jnp.bfloat16)
    new_m[...] = m
    new_v[...] = v


def adamw(which, w, m, v, g, block=176):
    spec = pl.BlockSpec((block, 8, 128), lambda i: (i, 0, 0))
    return pl.pallas_call(
        adamw_kernel,
        out_shape=[jax.ShapeDtypeStruct(a.shape, a.dtype) for a in (w, m, v)],
        grid=(w.shape[0] // block,),
        in_specs=[spec, spec, spec, pl.BlockSpec((1, block, 8, 128), lambda i: (which, i, 0, 0))],
        out_specs=[spec] * 3,
        name="adamw",
    )(w, m, v, g)


def to_tiles(a):
    *lead, rows, columns = a.shape
    a = a.reshape(*lead, rows // 8, 8, columns // 128, 128)
    return jnp.swapaxes(a, -3, -2).reshape(-1, 8, 128)


def from_tiles(t, shape):
    *lead, rows, columns = shape
    t = t.reshape(*lead, rows // 8, columns // 128, 8, 128)
    return jnp.swapaxes(t, -3, -2).reshape(shape)


def solution(mesh):
    def step(x, dy, *arrays):
        weights, m, v = (arrays[i : i + 3] for i in (0, 3, 6))
        layers = weights[0].shape[0]
        h, kept = x[0], []
        for number in range(layers):
            kept.append(h)
            h = layer(h, {name: w[number] for name, w in zip(NAMES, weights, strict=True)})
        by_h, terms = dy[0], []
        for number in reversed(range(layers)):
            _, back = jax.vjp(lambda w, h: layer(h, w), {name: w[number] for name, w in zip(NAMES, weights, strict=True)}, kept[number])
            by_w, by_h = back(by_h)
            terms += [to_tiles(by_w[name]) for name in NAMES]
        summed = reduce_gradients(terms).reshape(3, layers * TILES, 8, 128)
        new = [adamw(i, to_tiles(w), to_tiles(m), to_tiles(v), summed) for i, (w, m, v) in enumerate(zip(weights, m, v, strict=True))]
        return tuple(from_tiles(one[which], w.shape) for which in range(3) for one, w in zip(new, weights, strict=True))

    return jax.shard_map(
        step,
        mesh=mesh,
        in_specs=(P(("rep", "dp"), None, None),) * 2 + (P(None, None, None),) * 9,
        out_specs=(P("rep", None, None),) * 9,
        check_vma=False,
    )
```

time: 764 us -> 552 us (0.72)
  waiting for transfers between devices: 428 us -> 0 us
  Pallas kernels: 0 us -> 352 us
  other arithmetic: 126 us -> 3.82 us
  between operations: 14.5 us -> 1.09 us
    psum x1 -> x0, waiting for transfers between devices: 428 us -> none  [step(): summed[number] = [lax.psum(by_w[name], 'dp') for name in NAMES]]
    pallas_call x0 -> x4, Pallas kernels: none -> 352 us  [the longest x1 195 us: reduce_gradients(): pl.pallas_call(reduce_kernel, out_shape=jax.ShapeDtypeStruct((MATRICES, T...]
    convert_element_type x2 -> x0, other arithmetic: 124 us -> none  [adamw(): return ((w - 0.02 * step).astype(jnp.bfloat16), m, v)]
  transfers between devices with their start and end apart: 1 -> 0, of which waited for: 1 -> 0; matrix products, arithmetic and copies ran while one was open for 0% -> 0% of each run, Pallas kernels for 0% -> 0%
where the time goes in v1:
time: 552 us; the launch traced here: 543 us
  Pallas kernels  352 us (64%)
  matrix products  180 us (33%)
  local copies, waits for them, and re-layouts  7.13 us (1%)
    pallas_call x1, Pallas kernels, reduce_gradients(): pl.pallas_call(reduce_kernel, out_shape=jax.ShapeDtypeStruct((MATRICES, T...  195 us
    pallas_call x3, Pallas kernels, adamw(): pl.pallas_call(adamw_kernel, out_shape=[jax.ShapeDtypeStruct(a.shape, a.d...  157 us
    dot_general x5, matrix products, layer(): gate = jnp.dot(a, w['w_gate'], preferred_element_type=jnp.float32)  65.5 us
    dot_general x5, matrix products, layer(): up = jnp.dot(a, w['w_up'], preferred_element_type=jnp.float32)  62.8 us
    dot_general x5, matrix products, matmul(): jnp.dot(a, w, preferred_element_type=jnp.float32).astype(jnp.bfloat16)  51.3 us

profile of v1, /device:TPU:1, one launch (start us, length us, event | category | flops | bytes accessed | tf_op | source)
XLA Modules:
  0.0 543.4 jit_solution(13318900636054157835)
XLA Ops:
  0.6 2.9 copy.20
  3.5 0.5 fusion.53
  4.0 4.2 copy.21
  8.2 11.1 %fusion.40 = bf16[1024,2816]{1,0:T(8,128)(2,1)} fusion(bf16[2,2816,1024]{2,1,0:T(8,128)(2,1)} %param.15, bf16[1,1024,1024]{2,1,0:T(8,128)(2,1)} %param.12), kind=kOutput, calls=%fused_computation.52 | convolution fusion | flops 5908463616 | bytes 13631488 | tf_op jit(solution)/shard_map/transpose(jvp())/dot_general | solution.py:304
  19.3 11.9 %fusion.29 = f32[1024,2816]{1,0:T(8,128)} fusion(bf16[2,1024,2816]{2,1,0:T(8,128)(2,1)} %param.13, bf16[1,1024,1024]{2,1,0:T(8,128)(2,1)S(1)} %copy-done.3, f32[1024]{0:T(1024)S(1)} %add_rsqrt_fusion), kind=kOutput, calls=%fused_computation.42 | convolution fusion | flops 5908725760 | bytes 19402752 | tf_op jit(solution)/shard_map/dot_general | solution.py:315
  31.2 15.2 %multiply_convert_fusion.1 = (bf16[1024,2816]{1,0:T(8,128)(2,1)}, f32[1024,2816]{1,0:T(8,128)}) fusion(f32[1024,2816]{1,0:T(8,128)} %fusion.29, bf16[2,1024,2816]{2,1,0:T(8,128)(2,1)} %param.14, bf16[1,1024,1024]{2,1,0:T(8,128)(2,1)} %param.11, f32[1024]{0:T(1024)S(1)} %add_rsqrt_fusion), kind=kOutput, calls=%fused_computation.17 | convolution fusion | flops 5926027264 | bytes 36704256 | tf_op jit(solution)/shard_map/dot_general | solution.py:316
  46.4 9.5 %fusion.57 = (f32[1024]{0:T(1024)S(1)}, bf16[1024,1024]{0,1:T(8,128)(2,1)}) fusion(bf16[1024,2816]{1,0:T(8,128)(2,1)} %get-tuple-element.27, bf16[2,2816,1024]{2,1,0:T(8,128)(2,1)S(1)} %bitcast.198, bf16[1,1024,1024]{1,2,0:T(8,128)(2,1)S(1)} %copy.20), kind=kOutput, calls=%fused_computation.69 | convolution fusion | flops 5910821888 | bytes 15732736 | tf_op jit(solution)/shard_map/dot_general | solution.py:304
  55.9 12.0 %fusion.19 = f32[1024,2816]{1,0:T(8,128)} fusion(bf16[2,1024,2816]{2,1,0:T(8,128)(2,1)} %param.14, bf16[1024,1024]{0,1:T(8,128)(2,1)} %get-tuple-element.30, f32[1024]{0:T(1024)S(1)} %fusion.77), kind=kOutput, calls=%fused_computation.32 | convolution fusion | flops 5908725760 | bytes 19402752 | tf_op jit(solution)/shard_map/jvp()/dot_general | solution.py:316
  67.9 20.7 %fusion.2 = (bf16[1024,2816]{1,0:T(8,128)(2,1)}, f32[1024,2816]{1,0:T(8,128)}) fusion(f32[1024,2816]{1,0:T(8,128)} %fusion.19, bf16[1024,2816]{1,0:T(8,128)(2,1)} %fusion.40, bf16[2,1024,2816]{2,1,0:T(8,128)(2,1)} %param.13, bf16[1024,1024]{0,1:T(8,128)(2,1)} %get-tuple-element.30, f32[1024]{0:T(1024)S(1)} %fusion.77), kind=kOutput, calls=%fused_computation.8 | convolution fusion | flops 5943328768 | bytes 42471424 | tf_op jit(solution)/shard_map/jvp()/dot_general | solution.py:315
  88.6 13.1 %fusion.43 = bf16[2816,1024]{1,0:T(8,128)(2,1)} fusion(f32[1024,2816]{1,0:T(8,128)} %fusion.19, bf16[1,1024,1024]{2,1,0:T(8,128)(2,1)S(1)} %copy-done.4, f32[1024,2816]{1,0:T(8,128)} %get-tuple-element.32), kind=kOutput, calls=%fused_computation.53 | convolution fusion | flops 5925765120 | bytes 30932992 | tf_op jit(solution)/shard_map/transpose(jvp())/dot_general | solution.py:304
  101.8 11.3 %fusion.11 = bf16[1024,1024]{0,1:T(8,128)(2,1)} fusion(bf16[1024,2816]{1,0:T(8,128)(2,1)} %fusion.40, bf16[2,1024,2816]{2,1,0:T(8,128)(2,1)S(1)} %bitcast.203, f32[1024,2816]{1,0:T(8,128)} %get-tuple-element.32), kind=kOutput, calls=%fused_computation.20 | convolution fusion | flops 5922881536 | bytes 25165824 | tf_op jit(solution)/shard_map/transpose(jvp())/dot_general | solution.py:316
  113.1 12.9 %fusion.35 = bf16[1024,2816]{1,0:T(8,128)(2,1)} fusion(bf16[1024,2816]{1,0:T(8,128)(2,1)} %fusion.40, bf16[1024,1024]{0,1:T(8,128)(2,1)} %get-tuple-element.30, f32[1024]{0:T(1024)S(1)} %fusion.77, f32[1024,2816]{1,0:T(8,128)} %get-tuple-element.32), kind=kOutput, calls=%fused_computation.48 | convolution fusion | flops 5928910848 | bytes 25169920 | tf_op jit(solution)/shard_map/transpose(jvp())/dot_general | solution.py:316
  126.1 9.1 %fusion.59 = (f32[1024]{0:T(1024)S(1)}, bf16[1024,1024]{0,1:T(8,128)(2,1)S(1)}) fusion(bf16[1024,1024]{0,1:T(8,128)(2,1)} %get-tuple-element.30, bf16[1024,1024]{0,1:T(8,128)(2,1)S(1)} %copy-done.7, bf16[1024,2816]{1,0:T(8,128)(2,1)S(1)} %bitcast.221, bf16[2,1024,2816]{2,1,0:T(8,128)(2,1)} %param.13), kind=kOutput, calls=%fused_computation.71 | convolution fusion | flops 5910821888 | bytes 17829888 | tf_op jit(solution)/shard_map/transpose(jvp())/dot_general | solution.py:315
  135.2 10.2 %convolution_convert_fusion = bf16[1024,2816]{1,0:T(8,128)(2,1)} fusion(bf16[1024,2816]{1,0:T(8,128)(2,1)S(1)} %bitcast.221, bf16[1024,1024]{0,1:T(8,128)(2,1)} %get-tuple-element.30, f32[1024]{0:T(1024)S(1)} %fusion.77), kind=kOutput, calls=%fused_computation.50 | convolution fusion | flops 5908725760 | bytes 13635584 | tf_op jit(solution)/shard_map/transpose(jvp())/dot_general | solution.py:315
  145.4 3.3 fusion.61
  148.7 0.0 slice-start.4
  148.7 10.8 %convolution_convert_fusion.1 = bf16[2816,1024]{1,0:T(8,128)(2,1)} fusion(bf16[1024,2816]{1,0:T(8,128)(2,1)} %get-tuple-element.27, bf16[1024,1024]{0,1:T(8,128)(2,1)S(1)} %fusion.61), kind=kOutput, calls=%fused_computation.55 | convolution fusion | flops 5908463616 | bytes 13631488 | tf_op jit(solution)/shard_map/transpose(jvp())/dot_general | solution.py:304
  159.6 6.7 %fusion.37 = bf16[1024,2816]{1,0:T(8,128)(2,1)S(1)} fusion(bf16[1024,1024]{0,1:T(8,128)(2,1)S(1)} %fusion.61, bf16[2,2816,1024]{2,1,0:T(8,128)(2,1)S(1)} %bitcast.200), kind=kOutput, calls=%fused_computation.51 | convolution fusion | flops 5908463616 | bytes 13631488 | tf_op jit(solution)/shard_map/transpose(jvp())/dot_general | solution.py:304
  166.3 13.6 %fusion.44 = bf16[1024,2816]{1,0:T(8,128)(2,1)} fusion(f32[1024,2816]{1,0:T(8,128)} %fusion.29, f32[1024,2816]{1,0:T(8,128)} %get-tuple-element.28, bf16[1024,2816]{1,0:T(8,128)(2,1)S(1)} %fusion.37, bf16[1,1024,1024]{1,2,0:T(8,128)(2,1)S(1)} %copy-done.2, f32[1024]{0:T(1024)S(1)} %copy-done.6), kind=kOutput, calls=%fused_computation.54 | convolution fusion | flops 5943328768 | bytes 36704256 | tf_op jit(solution)/shard_map/transpose(jvp())/dot_general | solution.py:315
  179.9 11.4 %fusion.36 = bf16[1024,2816]{1,0:T(8,128)(2,1)} fusion(bf16[1024,2816]{1,0:T(8,128)(2,1)S(1)} %fusion.37, f32[1024,2816]{1,0:T(8,128)} %fusion.29, bf16[1,1024,1024]{1,2,0:T(8,128)(2,1)S(1)} %copy-done.2, f32[1024]{0:T(1024)S(1)} %copy-done.6), kind=kOutput, calls=%fused_computation.49 | convolution fusion | flops 5928910848 | bytes 25169920 | tf_op jit(solution)/shard_map/transpose(jvp())/dot_general | solution.py:316
  191.3 194.8 %reduce_gradients.1 = bf16[6,2816,8,128]{3,2,1,0:T(8,128)(2,1)} custom-call(bf16[2816,8,128]{2,1,0:T(8,128)(2,1)} %bitcast.207, bf16[2816,8,128]{2,1,0:T(8,128)(2,1)} %bitcast.206, bf16[2816,8,128]{2,1,0:T(8,128)(2,1)} %bitcast.205, bf16[2816,8,128]{2,1,0:T(8,128)(2,1)} %bitcast.209, bf16[2816,8,128]{2,1,0:T(8,128)(2,1)} %bitcast.210, ...), custom_call_target="tpu_custom_call" | custom-call | tf_op jit(solution)/shard_map/reduce_gradients/pallas_call | solution.py:287
  386.1 52.4 %adamw.5 = (bf16[5632,8,128]{2,1,0:T(8,128)(2,1)}, f32[5632,8,128]{2,1,0:T(8,128)}, f32[5632,8,128]{2,1,0:T(8,128)}) custom-call(bf16[5632,8,128]{2,1,0:T(8,128)(2,1)} %bitcast.196, f32[5632,8,128]{2,1,0:T(8,128)} %bitcast.190, f32[5632,8,128]{2,1,0:T(8,128)} %bitcast.191, bf16[3,5632,8,128]{3,2,1,0:T(8,128)(2,1)} %bitcast.187), custom_call_target="tpu_custom_call" | custom-call | tf_op jit(solution)/shard_map/adamw/pallas_call | solution.py:333
  438.5 52.3 %adamw.4 = (bf16[5632,8,128]{2,1,0:T(8,128)(2,1)}, f32[5632,8,128]{2,1,0:T(8,128)}, f32[5632,8,128]{2,1,0:T(8,128)}) custom-call(bf16[5632,8,128]{2,1,0:T(8,128)(2,1)} %bitcast.201, f32[5632,8,128]{2,1,0:T(8,128)} %bitcast.192, f32[5632,8,128]{2,1,0:T(8,128)} %bitcast.193, bf16[3,5632,8,128]{3,2,1,0:T(8,128)(2,1)} %bitcast.188), custom_call_target="tpu_custom_call" | custom-call | tf_op jit(solution)/shard_map/adamw/pallas_call | solution.py:333
  490.8 52.3 %adamw.3 = (bf16[5632,8,128]{2,1,0:T(8,128)(2,1)}, f32[5632,8,128]{2,1,0:T(8,128)}, f32[5632,8,128]{2,1,0:T(8,128)}) custom-call(bf16[5632,8,128]{2,1,0:T(8,128)(2,1)} %bitcast.204, f32[5632,8,128]{2,1,0:T(8,128)} %bitcast.194, f32[5632,8,128]{2,1,0:T(8,128)} %bitcast.195, bf16[3,5632,8,128]{3,2,1,0:T(8,128)(2,1)} %bitcast.189), custom_call_target="tpu_custom_call" | custom-call | tf_op jit(solution)/shard_map/adamw/pallas_call | solution.py:333
  (44 shorter events, 0.1 us)
Async XLA Ops:
  3.5 42.9 %copy-start.1 = (bf16[1,1024,1024]{1,2,0:T(8,128)(2,1)}, bf16[1,1024,1024]{1,2,0:T(8,128)(2,1)S(1)}, u32[]{:S(2)}) copy-start(bf16[1,1024,1024]{1,2,0:T(8,128)(2,1)S(1)} %copy.20) | copy-start | bytes 6291460
  4.0 27.1 %copy-start.5 = (f32[1024]{0:T(1024)}, f32[1024]{0:T(1024)S(1)}, u32[]{:S(2)}) copy-start(f32[1024]{0:T(1024)S(1)} %add_rsqrt_fusion) | copy-start | bytes 12292
  8.2 11.1 %copy-start.3 = (bf16[1,1024,1024]{2,1,0:T(8,128)(2,1)S(1)}, bf16[1,1024,1024]{2,1,0:T(8,128)(2,1)}, u32[]{:S(2)}) copy-start(bf16[1,1024,1024]{2,1,0:T(8,128)(2,1)} %param.11) | copy-start | bytes 6291460
  19.3 27.1 %slice-start = ((s8[11534336]{0:T(1024)(128)(4,1)}), s8[4194304]{0:T(1024)(128)(4,1)S(1)}, s32[]{:S(2)}) async-start(s8[11534336]{0:T(1024)(128)(4,1)} %bitcast.197), calls=%async_computation | async-start | bytes 8388608
  31.2 15.2 %slice-start.1 = ((s8[11534336]{0:T(1024)(128)(4,1)}), s8[4194304]{0:T(1024)(128)(4,1)S(1)}, s32[]{:S(2)}) async-start(s8[11534336]{0:T(1024)(128)(4,1)} %bitcast.197), calls=%async_computation.1 | async-start | bytes 8388608
  31.2 15.2 %slice-start.2 = ((s8[11534336]{0:T(1024)(128)(4,1)}), s8[3145728]{0:T(1024)(128)(4,1)S(1)}, s32[]{:S(2)}) async-start(s8[11534336]{0:T(1024)(128)(4,1)} %bitcast.197), calls=%async_computation.2 | async-start | bytes 6291456
  67.9 20.7 %copy-start.4 = (bf16[1,1024,1024]{2,1,0:T(8,128)(2,1)S(1)}, bf16[1,1024,1024]{2,1,0:T(8,128)(2,1)}, u32[]{:S(2)}) copy-start(bf16[1,1024,1024]{2,1,0:T(8,128)(2,1)} %param.12) | copy-start | bytes 6291460
  67.9 33.8 %slice-start.6 = ((s8[11534336]{0:T(1024)(128)(4,1)}), s8[4194304]{0:T(1024)(128)(4,1)S(1)}, s32[]{:S(2)}) async-start(s8[11534336]{0:T(1024)(128)(4,1)} %bitcast.202), calls=%async_computation.6 | async-start | bytes 8388608
  67.9 33.8 %slice-start.7 = ((s8[11534336]{0:T(1024)(128)(4,1)}), s8[3145728]{0:T(1024)(128)(4,1)S(1)}, s32[]{:S(2)}) async-start(s8[11534336]{0:T(1024)(128)(4,1)} %bitcast.202), calls=%async_computation.7 | async-start | bytes 6291456
  88.6 13.1 %slice-start.8 = ((s8[11534336]{0:T(1024)(128)(4,1)}), s8[4194304]{0:T(1024)(128)(4,1)S(1)}, s32[]{:S(2)}) async-start(s8[11534336]{0:T(1024)(128)(4,1)} %bitcast.202), calls=%async_computation.8 | async-start | bytes 8388608
  101.8 24.3 %slice-start.9 = ((s8[5767168]{0:T(1024)(128)(4,1)}), s8[1572864]{0:T(1024)(128)(4,1)S(1)}, s32[]{:S(2)}) async-start(s8[5767168]{0:T(1024)(128)(4,1)} %bitcast.220), calls=%async_computation.9 | async-start | bytes 3145728
  113.1 13.0 %slice-start.10 = ((s8[5767168]{0:T(1024)(128)(4,1)}), s8[4194304]{0:T(1024)(128)(4,1)S(1)}, s32[]{:S(2)}) async-start(s8[5767168]{0:T(1024)(128)(4,1)} %bitcast.220), calls=%async_computation.10 | async-start | bytes 8388608
  113.1 13.0 %copy-start.7 = (bf16[1024,1024]{0,1:T(8,128)(2,1)S(1)}, bf16[1024,1024]{0,1:T(8,128)(2,1)}, u32[]{:S(2)}) copy-start(bf16[1024,1024]{0,1:T(8,128)(2,1)} %fusion.11) | copy-start | bytes 6291460
  135.2 10.2 %copy-start = (bf16[1,1024,1024]{1,2,0:T(8,128)(2,1)S(1)}, bf16[1,1024,1024]{1,2,0:T(8,128)(2,1)}, u32[]{:S(2)}) copy-start(bf16[1,1024,1024]{1,2,0:T(8,128)(2,1)} %copy.21) | copy-start | bytes 6291460
  145.4 14.2 %slice-start.3 = ((s8[11534336]{0:T(1024)(128)(4,1)}), s8[4194304]{0:T(1024)(128)(4,1)S(1)}, s32[]{:S(2)}) async-start(s8[11534336]{0:T(1024)(128)(4,1)} %bitcast.199), calls=%async_computation.3 | async-start | bytes 8388608
  148.7 10.9 %slice-start.4 = ((s8[11534336]{0:T(1024)(128)(4,1)}), s8[4194304]{0:T(1024)(128)(4,1)S(1)}, s32[]{:S(2)}) async-start(s8[11534336]{0:T(1024)(128)(4,1)} %bitcast.199), calls=%async_computation.4 | async-start | bytes 8388608
  148.7 10.9 %slice-start.5 = ((s8[11534336]{0:T(1024)(128)(4,1)}), s8[3145728]{0:T(1024)(128)(4,1)S(1)}, s32[]{:S(2)}) async-start(s8[11534336]{0:T(1024)(128)(4,1)} %bitcast.199), calls=%async_computation.5 | async-start | bytes 6291456
  159.6 6.7 %copy-start.2 = (bf16[1,1024,1024]{1,2,0:T(8,128)(2,1)S(1)}, bf16[1,1024,1024]{1,2,0:T(8,128)(2,1)}, u32[]{:S(2)}) copy-start(bf16[1,1024,1024]{1,2,0:T(8,128)(2,1)} %copy-done.1) | copy-start | bytes 6291460
  159.6 6.7 %copy-start.6 = (f32[1024]{0:T(1024)S(1)}, f32[1024]{0:T(1024)}, u32[]{:S(2)}) copy-start(f32[1024]{0:T(1024)} %copy-done.5) | copy-start | bytes 12292

commit v2 on v1

--- a/solution.py
+++ b/solution.py
@@ -298,23 +298,171 @@
     )(*grads)
 
 
-NAMES = ("w_gate", "w_up", "w_down")
-
-def matmul(a, w):
-    return jnp.dot(a, w, preferred_element_type=jnp.float32).astype(jnp.bfloat16)
-
-
-def normed(h):
-    wide = h.astype(jnp.float32)
-    scale = lax.rsqrt(jnp.mean(wide**2, -1, keepdims=True) + 1e-6)
-    return (wide * scale).astype(jnp.bfloat16)
-
-
-def layer(h, w):
-    a = normed(h)
-    gate = jnp.dot(a, w["w_gate"], preferred_element_type=jnp.float32)
-    up = jnp.dot(a, w["w_up"], preferred_element_type=jnp.float32)
-    return h + matmul((jax.nn.silu(gate) * up).astype(jnp.bfloat16), w["w_down"])
+FF_BLOCK = 256
+
+
+def dot(a, b, contract=(1, 0)):
+    return lax.dot_general(a, b, (((contract[0],), (contract[1],)), ((), ())), preferred_element_type=jnp.float32)
+
+
+ROWS = 128
+
+
+def by_rows(total, body):
+    lax.fori_loop(0, total // ROWS, lambda i, _: (body(pl.ds(pl.multiple_of(i * ROWS, ROWS), ROWS)), 0)[1], 0)
+
+
+def norm_rows(h, a, tokens):
+    def some(rows):
+        wide = h[0, rows, :].astype(jnp.float32)
+        scale = lax.rsqrt(jnp.mean(wide**2, -1, keepdims=True) + 1e-6)
+        a[rows, :] = (wide * scale).astype(jnp.bfloat16)
+
+    by_rows(tokens, some)
+
+
+def forward_kernel(h, w_gate, w_up, w_down, gate_out, up_out, h_out, a, total):
+    step = pl.program_id(0)
+    tokens = a.shape[0]
+
+    @pl.when(step == 0)
+    def _():
+        norm_rows(h, a, tokens)
+
+    gate = dot(a[...], w_gate[0])
+    up = dot(a[...], w_up[0])
+    gate_out[...] = gate
+    up_out[...] = up
+    hidden = (gate * jax.nn.sigmoid(gate) * up).astype(jnp.bfloat16)
+    part = dot(hidden, w_down[0])
+
+    @pl.when(step == 0)
+    def _():
+        total[...] = part
+
+    @pl.when(step > 0)
+    def _():
+        total[...] += part
+
+    @pl.when(step == pl.num_programs(0) - 1)
+    def _():
+        def some(rows):
+            h_out[0, rows, :] = (h[0, rows, :].astype(jnp.float32) + total[rows, :].astype(jnp.bfloat16).astype(jnp.float32)).astype(jnp.bfloat16)
+
+        by_rows(tokens, some)
+
+
+def hidden_backward(gate, up, by_hidden):
+    s = jax.nn.sigmoid(gate)
+    act = gate * s
+    by_hidden = by_hidden.astype(jnp.bfloat16).astype(jnp.float32)
+    hidden = (act * up).astype(jnp.bfloat16)
+    by_up = (by_hidden * act).astype(jnp.bfloat16)
+    by_gate = (by_hidden * up * (s * (1 + gate * (1 - s)))).astype(jnp.bfloat16)
+    return hidden, by_gate, by_up
+
+
+def last_layer_kernel(h, dy, w_gate, w_up, w_down, g_gate, g_up, g_down, h_out, a, a_t, total):
+    step = pl.program_id(0)
+    tokens = a.shape[0]
+
+    @pl.when(step == 0)
+    def _():
+        norm_rows(h, a, tokens)
+        a_t[...] = a[...].T
+
+    gate = dot(a[...], w_gate[0])
+    up = dot(a[...], w_up[0])
+    by_hidden = dot(dy[0], w_down[0], (1, 1))
+    hidden, by_gate, by_up = hidden_backward(gate, up, by_hidden)
+    g_down[...] = dot(hidden, dy[0], (0, 0)).astype(jnp.bfloat16)
+    g_gate[...] = dot(a_t[...], by_gate).astype(jnp.bfloat16)
+    g_up[...] = dot(a_t[...], by_up).astype(jnp.bfloat16)
+    part = dot(by_gate, w_gate[0], (1, 1)) + dot(by_up, w_up[0], (1, 1))
+
+    @pl.when(step == 0)
+    def _():
+        total[...] = part
+
+    @pl.when(step > 0)
+    def _():
+        total[...] += part
+
+    @pl.when(step == pl.num_programs(0) - 1)
+    def _():
+        width = a.shape[1]
+
+        def some(rows):
+            wide = h[0, rows, :].astype(jnp.float32)
+            by_a = total[rows, :].astype(jnp.bfloat16).astype(jnp.float32)
+            scale = lax.rsqrt(jnp.mean(wide**2, -1, keepdims=True) + 1e-6)
+            along = jnp.sum(by_a * wide, -1, keepdims=True)
+            by_wide = by_a * scale - wide * (scale * scale * scale * along * (1.0 / width))
+            h_out[0, rows, :] = (dy[0, rows, :].astype(jnp.float32) + by_wide.astype(jnp.bfloat16).astype(jnp.float32)).astype(jnp.bfloat16)
+
+        by_rows(tokens, some)
+
+
+def first_layer_kernel(h, by_h, gate, up, w_down, g_gate, g_up, g_down, a, a_t):
+    @pl.when(pl.program_id(0) == 0)
+    def _():
+        norm_rows(h, a, a.shape[0])
+        a_t[...] = a[...].T
+
+    by_hidden = dot(by_h[0], w_down[0], (1, 1))
+    hidden, by_gate, by_up = hidden_backward(gate[...], up[...], by_hidden)
+    g_down[...] = dot(hidden, by_h[0], (0, 0)).astype(jnp.bfloat16)
+    g_gate[...] = dot(a_t[...], by_gate).astype(jnp.bfloat16)
+    g_up[...] = dot(a_t[...], by_up).astype(jnp.bfloat16)
+
+
+def forward_and_backward(x, dy, w_gate, w_up, w_down):
+    _, tokens, d = x.shape
+    ff = w_gate.shape[2]
+    block = FF_BLOCK
+    grid = (ff // block,)
+    whole = pl.BlockSpec((1, tokens, d), lambda i: (0, 0, 0), pipeline_mode=pl.Buffered(1))
+    wide = lambda n: pl.BlockSpec((1, d, block), lambda i: (n, 0, i))
+    tall = lambda n: pl.BlockSpec((1, block, d), lambda i: (n, i, 0))
+    hidden = pl.BlockSpec((tokens, block), lambda i: (0, i))
+    g_specs = [pl.BlockSpec((d, block), lambda i: (0, i))] * 2 + [pl.BlockSpec((block, d), lambda i: (i, 0))]
+    bf, f32 = jnp.bfloat16, jnp.float32
+    g_shapes = [jax.ShapeDtypeStruct((d, ff), bf)] * 2 + [jax.ShapeDtypeStruct((ff, d), bf)]
+    states = pltpu.VMEM((tokens, d), bf)
+    turned = pltpu.VMEM((d, tokens), bf)
+    sums = pltpu.VMEM((tokens, d), f32)
+    params = pltpu.CompilerParams(vmem_limit_bytes=56 * 2**20)
+    gate, up, h = pl.pallas_call(
+        forward_kernel,
+        out_shape=[jax.ShapeDtypeStruct((tokens, ff), f32)] * 2 + [jax.ShapeDtypeStruct(x.shape, bf)],
+        grid=grid,
+        in_specs=[whole, wide(0), wide(0), tall(0)],
+        out_specs=[hidden, hidden, whole],
+        scratch_shapes=[states, sums],
+        compiler_params=params,
+        name="first_layer_forward",
+    )(x, w_gate, w_up, w_down)
+    *last, by_h = pl.pallas_call(
+        last_layer_kernel,
+        out_shape=g_shapes + [jax.ShapeDtypeStruct(x.shape, bf)],
+        grid=grid,
+        in_specs=[whole, whole, wide(1), wide(1), tall(1)],
+        out_specs=g_specs + [whole],
+        scratch_shapes=[states, turned, sums],
+        compiler_params=params,
+        name="last_layer",
+    )(h, dy, w_gate, w_up, w_down)
+    first = pl.pallas_call(
+        first_layer_kernel,
+        out_shape=g_shapes,
+        grid=grid,
+        in_specs=[whole, whole, hidden, hidden, tall(0)],
+        out_specs=g_specs,
+        scratch_shapes=[states, turned],
+        compiler_params=params,
+        name="first_layer_backward",
+    )(x, by_h, gate, up, w_down)
+    return [*last, *first]
 
 
 def adamw_kernel(w, m, v, g, new_w, new_m, new_v):
@@ -328,7 +476,7 @@
     new_v[...] = v
 
 
-def adamw(which, w, m, v, g, block=176):
+def adamw(which, w, m, v, g, block=704):
     spec = pl.BlockSpec((block, 8, 128), lambda i: (i, 0, 0))
     return pl.pallas_call(
         adamw_kernel,
@@ -336,6 +484,7 @@
         grid=(w.shape[0] // block,),
         in_specs=[spec, spec, spec, pl.BlockSpec((1, block, 8, 128), lambda i: (which, i, 0, 0))],
         out_specs=[spec] * 3,
+        compiler_params=pltpu.CompilerParams(vmem_limit_bytes=56 * 2**20),
         name="adamw",
     )(w, m, v, g)
 
@@ -355,17 +504,8 @@
 def solution(mesh):
     def step(x, dy, *arrays):
         weights, m, v = (arrays[i : i + 3] for i in (0, 3, 6))
-        layers = weights[0].shape[0]
-        h, kept = x[0], []
-        for number in range(layers):
-            kept.append(h)
-            h = layer(h, {name: w[number] for name, w in zip(NAMES, weights, strict=True)})
-        by_h, terms = dy[0], []
-        for number in reversed(range(layers)):
-            _, back = jax.vjp(lambda w, h: layer(h, w), {name: w[number] for name, w in zip(NAMES, weights, strict=True)}, kept[number])
-            by_w, by_h = back(by_h)
-            terms += [to_tiles(by_w[name]) for name in NAMES]
-        summed = reduce_gradients(terms).reshape(3, layers * TILES, 8, 128)
+        terms = [to_tiles(g) for g in forward_and_backward(x, dy, *weights)]
+        summed = reduce_gradients(terms).reshape(3, 2 * TILES, 8, 128)
         new = [adamw(i, to_tiles(w), to_tiles(m), to_tiles(v), summed) for i, (w, m, v) in enumerate(zip(weights, m, v, strict=True))]
         return tuple(from_tiles(one[which], w.shape) for which in range(3) for one, w in zip(new, weights, strict=True))
 

time: 552 us -> 444 us (0.80); the launches traced: 543 us -> 444 us
  matrix products: 180 us -> 0 us
  Pallas kernels: 352 us -> 443 us
  local copies, waits for them, and re-layouts: 7.13 us -> 0 us
    dot_general x15 -> x0, matrix products: 180 us -> none  [the longest x5 65.5 us: layer(): gate = jnp.dot(a, w['w_gate'], preferred_element_type=jnp.float32)]
    pallas_call x0 -> x3, Pallas kernels: none -> 129 us  [the longest x1 64.2 us: forward_and_backward(): pl.pallas_call(last_layer_kernel, out_shape=g_shapes + [jax.ShapeDtypeStr...]
    pallas_call x3, Pallas kernels: 157 us -> 120 us  [adamw(): pl.pallas_call(adamw_kernel, out_shape=[jax.ShapeDtypeStruct(a.shape, a.d...]
    unnamed x40 -> x0, local copies, waits for them, and re-layouts: 7.13 us -> none
where the time goes in v2:
time: 444 us
  Pallas kernels  443 us (100%)
    pallas_call x1, Pallas kernels, reduce_gradients(): pl.pallas_call(reduce_kernel, out_shape=jax.ShapeDtypeStruct((MATRICES, T...  195 us
    pallas_call x3, Pallas kernels, adamw(): pl.pallas_call(adamw_kernel, out_shape=[jax.ShapeDtypeStruct(a.shape, a.d...  120 us
    pallas_call x1, Pallas kernels, forward_and_backward(): pl.pallas_call(last_layer_kernel, out_shape=g_shapes + [jax.ShapeDtypeStr...  64.2 us
    pallas_call x1, Pallas kernels, forward_and_backward(): pl.pallas_call(first_layer_kernel, out_shape=g_shapes, grid=grid, in_spec...  34.2 us
    pallas_call x1, Pallas kernels, forward_and_backward(): pl.pallas_call(forward_kernel, out_shape=[jax.ShapeDtypeStruct((tokens, f...  30.5 us

profile of v2, /device:TPU:1, one launch (start us, length us, event | category | flops | bytes accessed | tf_op | source)
XLA Modules:
  0.0 443.6 jit_solution(885623906954290150)
XLA Ops:
  0.6 30.5 %first_layer_forward.1 = (f32[1024,2816]{1,0:T(8,128)}, f32[1024,2816]{1,0:T(8,128)}, bf16[1,1024,1024]{2,1,0:T(8,128)(2,1)}) custom-call(bf16[1,1024,1024]{2,1,0:T(8,128)(2,1)} %h.3, bf16[2,1024,2816]{2,1,0:T(8,128)(2,1)} %w_gate.3, bf16[2,1024,2816]{2,1,0:T(8,128)(2,1)} %w_up.3, bf16[2,2816,1024]{2,1,0:T(8,128)(2,1)} %w_down.5), custom_call_target="tpu_custom_call" | custom-call | tf_op jit(solution)/shard_map/first_layer_forward/pallas_call | solution.py:435
  31.2 64.2 %last_layer.1 = (bf16[1024,2816]{1,0:T(8,128)(2,1)}, bf16[1024,2816]{1,0:T(8,128)(2,1)}, bf16[2816,1024]{1,0:T(8,128)(2,1)}, bf16[1,1024,1024]{2,1,0:T(8,128)(2,1)}) custom-call(bf16[1,1024,1024]{2,1,0:T(8,128)(2,1)} %get-tuple-element.28.h, bf16[1,1024,1024]{2,1,0:T(8,128)(2,1)} %dy.1, bf16[2,1024,2816]{2,1,0:T(8,128)(2,1)} %w_gate.3, ...), custom_call_target="tpu_custom_call" | custom-call | tf_op jit(solution)/shard_map/last_layer/pallas_call | solution.py:445
  95.3 34.2 %first_layer_backward.1 = (bf16[1024,2816]{1,0:T(8,128)(2,1)}, bf16[1024,2816]{1,0:T(8,128)(2,1)}, bf16[2816,1024]{1,0:T(8,128)(2,1)}) custom-call(bf16[1,1024,1024]{2,1,0:T(8,128)(2,1)} %h.3, bf16[1,1024,1024]{2,1,0:T(8,128)(2,1)} %get-tuple-element.32.by_h, f32[1024,2816]{1,0:T(8,128)} %get-tuple-element.33.gate, f32[1024,2816]{1,0:T(8,128)} %get-tuple-element.34.up, ...), custom_call_target="tpu_custom_call" | custom-call | tf_op jit(solution)/shard_map/first_layer_backward/pallas_call | solution.py:455
  129.5 194.5 %reduce_gradients.1 = bf16[6,2816,8,128]{3,2,1,0:T(8,128)(2,1)} custom-call(bf16[2816,8,128]{2,1,0:T(8,128)(2,1)} %bitcast.133, bf16[2816,8,128]{2,1,0:T(8,128)(2,1)} %bitcast.134, bf16[2816,8,128]{2,1,0:T(8,128)(2,1)} %bitcast.135, bf16[2816,8,128]{2,1,0:T(8,128)(2,1)} %bitcast.136, bf16[2816,8,128]{2,1,0:T(8,128)(2,1)} %bitcast.137, ...), custom_call_target="tpu_custom_call" | custom-call | tf_op jit(solution)/shard_map/reduce_gradients/pallas_call | solution.py:287
  324.0 39.9 %adamw.5 = (bf16[5632,8,128]{2,1,0:T(8,128)(2,1)}, f32[5632,8,128]{2,1,0:T(8,128)}, f32[5632,8,128]{2,1,0:T(8,128)}) custom-call(bf16[5632,8,128]{2,1,0:T(8,128)(2,1)} %bitcast.124, f32[5632,8,128]{2,1,0:T(8,128)} %bitcast.127, f32[5632,8,128]{2,1,0:T(8,128)} %bitcast.128, bf16[3,5632,8,128]{3,2,1,0:T(8,128)(2,1)} %bitcast.121), custom_call_target="tpu_custom_call" | custom-call | tf_op jit(solution)/shard_map/adamw/pallas_call | solution.py:481
  363.9 39.9 %adamw.4 = (bf16[5632,8,128]{2,1,0:T(8,128)(2,1)}, f32[5632,8,128]{2,1,0:T(8,128)}, f32[5632,8,128]{2,1,0:T(8,128)}) custom-call(bf16[5632,8,128]{2,1,0:T(8,128)(2,1)} %bitcast.125, f32[5632,8,128]{2,1,0:T(8,128)} %bitcast.129, f32[5632,8,128]{2,1,0:T(8,128)} %bitcast.130, bf16[3,5632,8,128]{3,2,1,0:T(8,128)(2,1)} %bitcast.122), custom_call_target="tpu_custom_call" | custom-call | tf_op jit(solution)/shard_map/adamw/pallas_call | solution.py:481
  403.8 39.9 %adamw.3 = (bf16[5632,8,128]{2,1,0:T(8,128)(2,1)}, f32[5632,8,128]{2,1,0:T(8,128)}, f32[5632,8,128]{2,1,0:T(8,128)}) custom-call(bf16[5632,8,128]{2,1,0:T(8,128)(2,1)} %bitcast.126, f32[5632,8,128]{2,1,0:T(8,128)} %bitcast.131, f32[5632,8,128]{2,1,0:T(8,128)} %bitcast.132, bf16[3,5632,8,128]{3,2,1,0:T(8,128)(2,1)} %bitcast.123), custom_call_target="tpu_custom_call" | custom-call | tf_op jit(solution)/shard_map/adamw/pallas_call | solution.py:481

commit v3 on v0

v3 whole, which is shorter than its diff:
```python
import jax
import jax.numpy as jnp
from jax import lax
from jax.experimental import pallas as pl
from jax.experimental.pallas import tpu as pltpu
from jax.sharding import PartitionSpec as P

MESH = pl.DeviceIdType.MESH
BF16, F32 = jnp.bfloat16, jnp.float32

BLOCK = 256
BLOCKS = 11
UNITS = 11
HALF = 768
SIZE = {"x": 4, "y": 4, "z": 8}
COLORS = []
_start = 0
_rings = [0, 2, 4, 5, 6, 7, 8, 9, 10, 12, 14]
for _axes, _slots in (("xyz", _rings), ("yxz", _rings), ("zxy", list(range(15)))):
    _n3 = 2
    _n2 = _n3 * SIZE[_axes[2]]
    _n1 = _n2 * SIZE[_axes[1]]
    COLORS.append((_axes, _start, (_n1, _n2, _n3), _slots))
    _start += _n1 * SIZE[_axes[0]]
assert _start == HALF
FIN_SLOT, SWAP_SLOT, END_SLOT = 7, 15, 16
HELD = 6
PACE = 3
LAST_CALLS, FIRST_CALLS = 4, 2
COMPUTE_CALLS = BLOCKS * (LAST_CALLS + FIRST_CALLS)


def ready(m):
    return jnp.where(m < 5, 8 * m + 8, jnp.where(m == 5, 46, 4 * m + 26))


CALLS = COMPUTE_CALLS + PACE * (END_SLOT + 1) + 1


def ring_slots(n, hops):
    slots, at = [], 0
    for hop in range(hops):
        row = []
        for way in range(2):
            first = n - n // 2 if way == 0 else n // 2
            size = first if hop == 0 else n
            row.append((at, size))
            at += size
        slots.append(row)
    return slots, at


class Layout:
    def __init__(self):
        self.r1, self.r2, self.r3, self.s3, self.fin, self.sem = [], [], [], [], [], {}
        a1 = a2 = a3 = s3 = fin = sems = 0
        for c, (axes, _, (n1, n2, n3), _) in enumerate(COLORS):
            h1, h2, k3 = SIZE[axes[0]] // 2, SIZE[axes[1]] // 2, SIZE[axes[2]]
            slots, size = ring_slots(n1, h1)
            self.r1.append([[(a1 + s, n) for s, n in row] for row in slots])
            a1 += size
            slots, size = ring_slots(n2, h2)
            self.r2.append([[(a2 + s, n) for s, n in row] for row in slots])
            a2 += size
            self.r3.append(a3)
            a3 += (k3 - 1) * n3
            self.s3.append(s3)
            s3 += n2
            self.fin.append(fin)
            fin += n3
            for kind, count in (("r1", 2 * h1), ("r2", 2 * h2), ("r3", 1), ("g3", 1), ("g2", 2 * h2), ("g1", 2 * h1)):
                self.sem[c, kind] = sems
                sems += count
        self.n1, self.n2, self.n3, self.ns, self.nf, self.sems = a1, a2, a3, s3, fin, sems


LAY = Layout()
SENT = HALF + LAY.n1 + LAY.n2 + LAY.n3


def add_tiles(dst, dst_at, size, terms, chunk=8):
    def some(at, n):
        total = None
        for ref, start in terms:
            value = ref[pl.ds(start + at, n)].astype(F32)
            total = value if total is None else total + value
        dst[pl.ds(dst_at + at, n)] = total.astype(BF16)

    full = size // chunk
    if full > 1:
        lax.fori_loop(0, full, lambda i, _: (some(i * chunk, chunk), 0)[1], 0)
    elif full == 1:
        some(0, chunk)
    if size % chunk:
        some(full * chunk, size % chunk)


def remote(src, dst, send, receive, to):
    return pltpu.make_async_remote_copy(src_ref=src, dst_ref=dst, send_sem=send, recv_sem=receive, device_id=to, device_id_type=MESH)


def arrived(ref, n, sem):
    pltpu.make_async_copy(ref.at[pl.ds(0, n)], ref.at[pl.ds(0, n)], sem).wait()


class Engine:
    def __init__(self, terms, out, own, par, r1, r2, r3, s3, fin, send_rs, send_ag, recv, pair, load, written, credit):
        self.terms, self.out, self.own, self.par, self.r1, self.r2, self.r3, self.s3, self.fin = terms, out, own, par, r1, r2, r3, s3, fin
        self.send_rs, self.send_ag, self.recv, self.pair, self.load, self.written, self.credit = send_rs, send_ag, recv, pair, load, written, credit
        me = lax.axis_index("dp")
        self.core = me % 2
        self.place = {"x": me // 64, "y": me // 16 % 4, "z": me // 2 % 8}
        self.peers = [self.device()] + [self.device("x", d) for d in (1, 3)]
        self.peers += [self.device("y", d) for d in (1, 2, 3)] + [self.device("z", d) for d in range(1, 8)]

    def device(self, axis=None, by=0):
        at = dict(self.place)
        core = self.core
        if axis is None:
            core = 1 - core
        else:
            at[axis] = (at[axis] + by + SIZE[axis]) % SIZE[axis]
        return (0, ((at["x"] * 4 + at["y"]) * 8 + at["z"]) * 2 + core)

    def greet(self):
        for peer in self.peers:
            pl.semaphore_signal(pltpu.get_barrier_semaphore(), inc=1, device_id=peer, device_id_type=MESH)

    def meet(self):
        pl.semaphore_wait(pltpu.get_barrier_semaphore(), len(self.peers))

    def begin(self, m):
        for half in range(2):
            arrived(self.out.at[0], HALF, self.written.at[half])

        @pl.when(m >= HELD)
        def _():
            pl.semaphore_wait(self.credit.at[m - HELD], len(self.peers))
            arrived(self.out.at[0], SENT, self.send_rs.at[m - HELD])

        unit = pl.ds(m * HALF, HALF)
        pltpu.make_async_copy(self.terms.at[self.core, unit], self.own.at[m % HELD], self.load.at[m, 0]).start()
        remote(self.terms.at[1 - self.core, unit], self.par.at[m % HELD], self.send_rs.at[m], self.pair.at[m, 0], self.device()).start()

    def color_stage(self, c, stage, m):
        axes, start, (n1, n2, n3), _ = COLORS[c]
        k1, k2, k3 = (SIZE[a] for a in axes)
        p1, p2, p3 = (self.place[a] for a in axes)
        h1, h2 = k1 // 2, k2 // 2
        b = m % HELD
        o, q, a1, a2, a3 = (ref.at[b] for ref in (self.own, self.par, self.r1, self.r2, self.r3))
        result, mine = self.out.at[self.core], m * HALF
        send_rs, send_ag, load = self.send_rs.at[m], self.send_ag.at[m], self.load.at[m, 1 + c]
        device = self.device
        base2 = start + p1 * n1
        base3 = base2 + p2 * n2
        shard = base3 + p3 * n3

        def sem(kind, i=0):
            return self.recv.at[m, LAY.sem[c, kind] + i]

        def ring_reduce(axis, k, p, n, base, hop, slots, arrivals, kind, more):
            h = k // 2
            j = h - hop
            for way, sign in ((0, 1), (1, -1)):
                owner = (p + sign * j + k) % k
                at = base + owner * n
                lo, size = (0, n) if j < h else ((0, n - n // 2) if way == 0 else (n - n // 2, n // 2))
                extra = [(ref, where + owner * n) for ref, where in more]
                if hop == 0:
                    add_tiles(o, at + lo, size, [(o, at + lo), (q, at + lo)] + [(r, w + lo) for r, w in extra])
                else:
                    there, got = slots[hop - 1][way]
                    arrived(arrivals, got, sem(kind, 2 * (hop - 1) + way))
                    if got == n:
                        add_tiles(o, at, n, [(o, at), (q, at)] + extra + [(arrivals, there)])
                    else:
                        first = 0 if way == 0 else n - got
                        add_tiles(o, at + first, got, [(o, at + first), (q, at + first)] + [(r, w + first) for r, w in extra] + [(arrivals, there)])
                        other, rest = (got, n - got) if way == 0 else (0, n - got)
                        add_tiles(o, at + other, rest, [(o, at + other), (q, at + other)] + [(r, w + other) for r, w in extra])
                there, size2 = slots[hop][way]
                assert size2 == size
                remote(o.at[pl.ds(at + lo, size)], arrivals.at[pl.ds(there, size)], send_rs, sem(kind, 2 * hop + way), device(axis, sign)).start()

        def ring_wait(h, slots, arrivals, kind):
            for way in range(2):
                arrived(arrivals, slots[h - 1][way][1], sem(kind, 2 * (h - 1) + way))

        def gather_sizes(k, n, hop):
            return [(0, n), (0, n)] if hop < k // 2 - 1 else [(0, n - n // 2), (n - n // 2, n // 2)]

        def gather_wait(k, n, hop, kind):
            for way in range(2):
                arrived(result, gather_sizes(k, n, hop)[way][1], sem(kind, 2 * hop + way))

        def ring_gather(axis, k, p, n, base, hop, kind):
            if hop:
                gather_wait(k, n, hop - 1, kind)
            for way, sign in ((0, 1), (1, -1)):
                lo, size = gather_sizes(k, n, hop)[way]
                piece = result.at[pl.ds(mine + base + (p - sign * hop + k) % k * n + lo, size)]
                remote(piece, piece, send_ag, sem(kind, 2 * hop + way), device(axis, sign)).start()

        last1 = [(a1, LAY.r1[c][h1 - 1][way][0]) for way in range(2)]
        last2 = [(a2, LAY.r2[c][h2 - 1][way][0]) for way in range(2)]
        if stage < h1:
            ring_reduce(axes[0], k1, p1, n1, start, stage, LAY.r1[c], a1, "r1", [])
            return
        stage -= h1
        if stage < h2:
            if stage == 0:
                ring_wait(h1, LAY.r1[c], a1, "r1")
            ring_reduce(axes[1], k2, p2, n2, base2, stage, LAY.r2[c], a2, "r2", last1)
            return
        stage -= h2
        if stage == 0:
            ring_wait(h2, LAY.r2[c], a2, "r2")
            add_tiles(self.s3.at[b], LAY.s3[c], n2, [(o, base3), (q, base3)] + [(r, w + p2 * n2) for r, w in last1] + last2)
            for d in range(1, k3):
                piece = self.s3.at[b, pl.ds(LAY.s3[c] + (p3 + d) % k3 * n3, n3)]
                remote(piece, a3.at[pl.ds(LAY.r3[c] + (d - 1) * n3, n3)], send_rs, sem("r3"), device(axes[2], d)).start()
            return
        stage -= 1
        if stage == 0:
            arrived(a3, (k3 - 1) * n3, sem("r3"))
            terms = [(o, shard), (q, shard)] + [(r, w + p2 * n2 + p3 * n3) for r, w in last1] + [(r, w + p3 * n3) for r, w in last2]
            terms += [(a3, LAY.r3[c] + (d - 1) * n3) for d in range(1, k3)]
            add_tiles(self.fin.at[m], LAY.fin[c], n3, terms)
            piece = self.fin.at[m, pl.ds(LAY.fin[c], n3)]
            there = result.at[pl.ds(mine + shard, n3)]
            pltpu.make_async_copy(piece, there, load).start()
            for d in range(1, k3):
                remote(piece, there, send_ag, sem("g3"), device(axes[2], d)).start()
            return
        stage -= 1
        if stage < h2:
            if stage == 0:
                arrived(result, n3, load)
                arrived(result, (k3 - 1) * n3, sem("g3"))
            ring_gather(axes[1], k2, p2, n2, base2, stage, "g2")
            return
        stage -= h2
        if stage < h1:
            if stage == 0:
                gather_wait(k2, n2, h2 - 1, "g2")
            ring_gather(axes[0], k1, p1, n1, start, stage, "g1")
            return
        gather_wait(k1, n1, h1 - 1, "g1")

    def slot(self, s, m):
        if s == -1:
            self.begin(m)
        if s == 0:
            arrived(self.out.at[0], HALF, self.load.at[m, 0])
            arrived(self.out.at[0], HALF, self.pair.at[m, 0])
        for c in (2, 0, 1):
            if s in COLORS[c][3]:
                self.color_stage(c, COLORS[c][3].index(s), m)
        if s == FIN_SLOT:

            @pl.when(m < UNITS - HELD)
            def _():
                for peer in self.peers:
                    pl.semaphore_signal(self.credit.at[m], inc=1, device_id=peer, device_id_type=MESH)

        if s == SWAP_SLOT:
            piece = self.out.at[self.core, pl.ds(m * HALF, HALF)]
            remote(piece, piece, self.send_ag.at[m], self.pair.at[m, 1], self.device()).start()
        if s == END_SLOT:
            arrived(self.out.at[0], HALF, self.pair.at[m, 1])
            arrived(self.out.at[0], SENT, self.send_ag.at[m])

    def step(self, call):
        def unit(m, _):
            since = call - ready(m)

            @pl.when((since >= 0) & (since <= PACE * (END_SLOT + 1)) & (since % PACE == 0))
            def _():
                s = since // PACE - 1
                for low in range(-1, END_SLOT + 1, 3):

                    @pl.when((s >= low) & (s < low + 3))
                    def _():
                        for one in range(low, min(low + 3, END_SLOT + 1)):
                            pl.when(s == one)(lambda one=one: self.slot(one, m))

            return 0

        lax.fori_loop(0, UNITS, unit, 0)

    def finish(self):
        def unit(m, _):
            arrived(self.out.at[0], SENT, self.send_rs.at[m])
            return 0

        lax.fori_loop(UNITS - HELD, UNITS, unit, 0)


def dot(a, b, contract=(1, 0)):
    return lax.dot_general(a, b, (((contract[0],), (contract[1],)), ((), ())), preferred_element_type=F32)


ROWS = 128


def by_rows(total, body):
    lax.fori_loop(0, total // ROWS, lambda i, _: (body(pl.ds(pl.multiple_of(i * ROWS, ROWS), ROWS)), 0)[1], 0)


def norm_rows(h, a):
    def some(rows):
        wide = h[0, rows, :].astype(F32)
        scale = lax.rsqrt(jnp.mean(wide**2, -1, keepdims=True) + 1e-6)
        a[rows, :] = (wide * scale).astype(BF16)

    by_rows(a.shape[0], some)


def forward_kernel(h, w_gate, w_up, w_down, gate_out, up_out, h_out, a_t, a, total):
    step = pl.program_id(0)

    @pl.when(step == 0)
    def _():
        norm_rows(h, a)
        a_t[...] = a[...].T

    gate = dot(a[...], w_gate[0])
    up = dot(a[...], w_up[0])
    gate_out[...] = gate
    up_out[...] = up
    hidden = (gate * jax.nn.sigmoid(gate) * up).astype(BF16)
    part = dot(hidden, w_down[0])

    @pl.when(step == 0)
    def _():
        total[...] = part

    @pl.when(step > 0)
    def _():
        total[...] += part

    @pl.when(step == pl.num_programs(0) - 1)
    def _():
        def some(rows):
            h_out[0, rows, :] = (h[0, rows, :].astype(F32) + total[rows, :].astype(BF16).astype(F32)).astype(BF16)

        by_rows(a.shape[0], some)


def hidden_backward(gate, up, by_hidden):
    s = jax.nn.sigmoid(gate)
    act = gate * s
    by_hidden = by_hidden.astype(BF16).astype(F32)
    hidden = (act * up).astype(BF16)
    by_up = (by_hidden * act).astype(BF16)
    by_gate = (by_hidden * up * (s * (1 + gate * (1 - s)))).astype(BF16)
    return hidden, by_gate, by_up


def backward_kernel(h, dy, first_a_t, w_gate, w_up, w_down, first_gate, first_up, out, terms, *scratch):
    a, a_t, total, by_h, gate, up, hidden, by_gate, by_up, grads, *held = scratch
    engine = Engine(terms, out, *held)
    written = engine.written
    step = pl.program_id(0)
    last, first = step < BLOCKS, (step >= BLOCKS) & (step < 2 * BLOCKS)
    slot = step % 2

    @pl.when(step == 0)
    def _():
        engine.greet()
        norm_rows(h, a)
        a_t[...] = a[...].T

    @pl.when(step == 1)
    def _():
        engine.meet()

    def send_off(which):
        for half in range(2):
            src = grads.at[slot, which, pl.ds(half * 128, 128)]
            pltpu.make_async_copy(src, terms.at[half, pl.ds((step * 3 + which) * 128, 128)], written.at[slot]).start()

    def keep(which, value):
        rows, columns = value.shape
        for i in range(columns // 128):
            grads[slot, which, pl.ds(i * (rows // 8), rows // 8)] = value[:, i * 128 : (i + 1) * 128].reshape(rows // 8, 8, 128).astype(BF16)

    def by_down(states):
        keep(2, dot(hidden[...], states, (0, 0)))
        send_off(2)

    def by_wide(turned):
        for which, ref in ((0, by_gate), (1, by_up)):
            keep(which, dot(turned, ref[...]))
            send_off(which)

    def part(k, _):
        engine.step(jnp.where(step < BLOCKS, step * LAST_CALLS, BLOCKS * LAST_CALLS + (step - BLOCKS) * FIRST_CALLS) + k)

        @pl.when(last & (k == 0))
        def _():
            gate[...] = dot(a[...], w_gate[0])
            up[...] = dot(a[...], w_up[0])

        @pl.when(last & (k == 1))
        def _():
            hidden[...], by_gate[...], by_up[...] = hidden_backward(gate[...], up[...], dot(dy[0], w_down[0], (1, 1)))
            by_down(dy[0])

        @pl.when(last & (k == 2))
        def _():
            by_wide(a_t[...])

        @pl.when(last & (k == 3))
        def _():
            for i in range(4):
                columns = pl.ds(i * 256, 256)
                value = dot(by_gate[...], w_gate[0, columns, :], (1, 1)) + dot(by_up[...], w_up[0, columns, :], (1, 1))
                total[:, columns] = jnp.where(step == 0, value, total[:, columns] + value)

        @pl.when((step == BLOCKS - 1) & (k == 3))
        def _():
            def some(rows):
                wide = h[0, rows, :].astype(F32)
                by_a = total[rows, :].astype(BF16).astype(F32)
                scale = lax.rsqrt(jnp.mean(wide**2, -1, keepdims=True) + 1e-6)
                along = jnp.sum(by_a * wide, -1, keepdims=True)
                by_wide = by_a * scale - wide * (scale * scale * scale * along * (1.0 / a.shape[1]))
                by_h[rows, :] = (dy[0, rows, :].astype(F32) + by_wide.astype(BF16).astype(F32)).astype(BF16)

            by_rows(a.shape[0], some)

        @pl.when(first & (k == 0))
        def _():
            hidden[...], by_gate[...], by_up[...] = hidden_backward(first_gate[...], first_up[...], dot(by_h[...], w_down[0], (1, 1)))
            by_down(by_h[...])

        @pl.when(first & (k == 1))
        def _():
            by_wide(first_a_t[...])

        return 0

    calls = jnp.where(last, LAST_CALLS, jnp.where(first, FIRST_CALLS, CALLS - COMPUTE_CALLS))
    lax.fori_loop(0, calls, part, 0)

    @pl.when(step == 2 * BLOCKS)
    def _():
        engine.finish()


def summed_gradients(x, dy, w_gate, w_up, w_down):
    _, tokens, d = x.shape
    ff = w_gate.shape[2]
    assert (tokens, d, ff) == (1024, 1024, BLOCKS * BLOCK)
    once = pl.Buffered(1)
    whole = pl.BlockSpec((1, tokens, d), lambda i: (0, 0, 0), pipeline_mode=once)
    turned = pl.BlockSpec((d, tokens), lambda i: (0, 0), pipeline_mode=once)
    wide = pl.BlockSpec((1, d, BLOCK), lambda i: (0, 0, i))
    tall = pl.BlockSpec((1, BLOCK, d), lambda i: (0, i, 0))
    hidden = pl.BlockSpec((tokens, BLOCK), lambda i: (0, i))
    vmem = lambda *shape, dtype=BF16: pltpu.VMEM(shape, dtype)
    gate, up, h, a_t = pl.pallas_call(
        forward_kernel,
        out_shape=[jax.ShapeDtypeStruct((tokens, ff), F32)] * 2 + [jax.ShapeDtypeStruct(x.shape, BF16), jax.ShapeDtypeStruct((d, tokens), BF16)],
        grid=(BLOCKS,),
        in_specs=[whole, wide, wide, tall],
        out_specs=[hidden, hidden, whole, turned],
        scratch_shapes=[vmem(tokens, d), vmem(tokens, d, dtype=F32)],
        compiler_params=pltpu.CompilerParams(vmem_limit_bytes=56 * 2**20),
        name="first_layer_forward",
    )(x, w_gate, w_up, w_down)
    before = lambda i: jnp.minimum(i, BLOCKS - 1)
    after = lambda i: jnp.clip(i - BLOCKS, 0, BLOCKS - 1)
    wide = pl.BlockSpec((1, d, BLOCK), lambda i: (1, 0, before(i)))
    tall = pl.BlockSpec((1, BLOCK, d), lambda i: (jnp.where(i < BLOCKS, 1, 0), jnp.where(i < BLOCKS, before(i), after(i)), 0))
    hidden = pl.BlockSpec((tokens, BLOCK), lambda i: (0, after(i)))
    tiles = lambda *n: vmem(*n, 8, 128)
    dma = pltpu.SemaphoreType.DMA
    total = jax.ShapeDtypeStruct((2, UNITS * HALF, 8, 128), BF16)
    summed, _ = pl.pallas_call(
        backward_kernel,
        out_shape=[total, total],
        grid=(2 * BLOCKS + 1,),
        in_specs=[whole, whole, turned, wide, wide, tall, hidden, hidden],
        out_specs=[pl.BlockSpec(memory_space=pl.ANY)] * 2,
        scratch_shapes=[
            vmem(tokens, d), vmem(d, tokens), vmem(tokens, d, dtype=F32), vmem(tokens, d),
            vmem(tokens, BLOCK, dtype=F32), vmem(tokens, BLOCK, dtype=F32), vmem(tokens, BLOCK), vmem(tokens, BLOCK), vmem(tokens, BLOCK),
            tiles(2, 3, 256),
            tiles(HELD, HALF), tiles(HELD, HALF), tiles(HELD, LAY.n1), tiles(HELD, LAY.n2), tiles(HELD, LAY.n3), tiles(HELD, LAY.ns), tiles(UNITS, LAY.nf),
            dma((UNITS,)), dma((UNITS,)), dma((UNITS, LAY.sems)), dma((UNITS, 2)), dma((UNITS, 4)), dma((2,)),
            pltpu.SemaphoreType.REGULAR((UNITS - HELD,)),
        ],
        compiler_params=pltpu.CompilerParams(collective_id=0, has_side_effects=True, vmem_limit_bytes=67043328),
        name="backward_and_sum",
    )(h, dy, a_t, w_gate, w_up, w_down, gate, up)
    return summed.reshape(2, 2 * BLOCKS, 3, 128, 8, 128)


def adamw_some(w, m, v, g, new_w, new_m, new_v, at, g_at):
    g = g[g_at].astype(F32)
    one = 0.9 * m[at] + 0.1 * g
    two = 0.95 * v[at] + 0.05 * g * g
    old = w[at].astype(F32)
    step = one * lax.rsqrt(two + 1e-8) + 0.1 * old
    new_w[at] = (old - 0.02 * step).astype(BF16)
    new_m[at] = one
    new_v[at] = two


def adamw_wide_kernel(*refs):
    for column in range(2 * BLOCKS):
        adamw_some(*refs, (0, slice(None), column), (column % 2, column // 2, 0))


def adamw_tall_kernel(*refs):
    for column in range(2):
        for block in range(BLOCKS):
            adamw_some(*refs, (0, slice(block * 32, (block + 1) * 32), column), (0, block, 0, column))


def adamw(which, w, m, v, summed):
    layers, rows, columns = w.shape[:3]
    if which < 2:
        some = 32
        grid = (layers, rows // some)
        spec = pl.BlockSpec((1, some, columns, 8, 128), lambda n, i: (n, i, 0, 0, 0))
        g, g_spec = summed, pl.BlockSpec((2, BLOCKS, 1, some, 8, 128), lambda n, i: (0, 1 - n, which, i, 0, 0))
        kernel = adamw_wide_kernel
    else:
        grid = (layers, columns // 2)
        spec = pl.BlockSpec((1, rows, 2, 8, 128), lambda n, i: (n, 0, i, 0, 0))
        g = summed.reshape(2, 2 * BLOCKS, 3, 4, 32, 8, 128)
        g_spec = pl.BlockSpec((1, BLOCKS, 1, 2, 32, 8, 128), lambda n, i: (i // 2, 1 - n, which, i % 2, 0, 0, 0))
        kernel = adamw_tall_kernel
    return pl.pallas_call(
        kernel,
        out_shape=[jax.ShapeDtypeStruct(a.shape, a.dtype) for a in (w, m, v)],
        grid=grid,
        in_specs=[spec, spec, spec, g_spec],
        out_specs=[spec] * 3,
        compiler_params=pltpu.CompilerParams(vmem_limit_bytes=56 * 2**20),
        name="adamw",
    )(w, m, v, g)


def to_tiles(a):
    *lead, rows, columns = a.shape
    return jnp.swapaxes(a.reshape(*lead, rows // 8, 8, columns // 128, 128), -3, -2)


def from_tiles(t):
    *lead, rows, columns, _, _ = t.shape
    return jnp.swapaxes(t, -3, -2).reshape(*lead, rows * 8, columns * 128)


def solution(mesh):
    def step(x, dy, *arrays):
        weights, m, v = (arrays[i : i + 3] for i in (0, 3, 6))
        summed = summed_gradients(x, dy, *weights)
        new = [adamw(i, *(to_tiles(one) for one in (w, m, v)), summed) for i, (w, m, v) in enumerate(zip(weights, m, v, strict=True))]
        return tuple(from_tiles(one[which]) for which in range(3) for one in new)

    return jax.shard_map(
        step,
        mesh=mesh,
        in_specs=(P(("rep", "dp"), None, None),) * 2 + (P(None, None, None),) * 9,
        out_specs=(P("rep", None, None),) * 9,
        check_vma=False,
    )
```

time: 764 us -> 402 us (0.53)
  waiting for transfers between devices: 428 us -> 0 us
  Pallas kernels: 0 us -> 401 us
  matrix products: 180 us -> 0 us
  other arithmetic: 126 us -> 0 us
  between operations: 14.5 us -> 0.66 us
  local copies, waits for them, and re-layouts: 7.88 us -> 0 us
    psum x1 -> x0, waiting for transfers between devices: 428 us -> none  [step(): summed[number] = [lax.psum(by_w[name], 'dp') for name in NAMES]]
    pallas_call x0 -> x5, Pallas kernels: none -> 401 us  [the longest x1 246 us: summed_gradients(): pl.pallas_call(backward_kernel, out_shape=[total, total], grid=(2 * BLOCK...]
    dot_general x15 -> x0, matrix products: 180 us -> none  [the longest x5 62.1 us: layer(): gate = jnp.dot(a, w['w_gate'], preferred_element_type=jnp.float32)]
    convert_element_type x2 -> x0, other arithmetic: 124 us -> none  [adamw(): return ((w - 0.02 * step).astype(jnp.bfloat16), m, v)]
    unnamed x42 -> x0, local copies, waits for them, and re-layouts: 7.88 us -> none
  transfers between devices with their start and end apart: 1 -> 0, of which waited for: 1 -> 0; matrix products, arithmetic and copies ran while one was open for 0% -> 0% of each run, Pallas kernels for 0% -> 0%
where the time goes in v3:
time: 402 us
  Pallas kernels  401 us (100%)
    pallas_call x1, Pallas kernels, summed_gradients(): pl.pallas_call(backward_kernel, out_shape=[total, total], grid=(2 * BLOCK...  246 us
    pallas_call x3, Pallas kernels, adamw(): pl.pallas_call(kernel, out_shape=[jax.ShapeDtypeStruct(a.shape, a.dtype)...  123 us
    pallas_call x1, Pallas kernels, summed_gradients(): pl.pallas_call(forward_kernel, out_shape=[jax.ShapeDtypeStruct((tokens, f...  31.9 us

profile of v3, /device:TPU:1, one launch (start us, length us, event | category | flops | bytes accessed | tf_op | source)
XLA Modules:
  0.0 401.6 jit_solution(10551632668727078303)
XLA Ops:
  0.6 31.9 %first_layer_forward.1 = (f32[1024,2816]{1,0:T(8,128)}, f32[1024,2816]{1,0:T(8,128)}, bf16[1,1024,1024]{2,1,0:T(8,128)(2,1)}, bf16[1024,1024]{1,0:T(8,128)(2,1)}) custom-call(bf16[1,1024,1024]{2,1,0:T(8,128)(2,1)} %h.1, bf16[2,1024,2816]{2,1,0:T(8,128)(2,1)} %w_gate.3, bf16[2,1024,2816]{2,1,0:T(8,128)(2,1)} %w_up.3, bf16[2,2816,1024]{2,1,0:T(8,128)(2,1)} %w_down.3), custom_call_target="tpu_custom_call" | custom-call | tf_op jit(solution)/shard_map/first_layer_forward/pallas_call | solution.py:464
  32.6 245.9 %backward_and_sum.1 = (bf16[2,8448,8,128]{3,2,1,0:T(8,128)(2,1)}, bf16[2,8448,8,128]{3,2,1,0:T(8,128)(2,1)}) custom-call(bf16[1,1024,1024]{2,1,0:T(8,128)(2,1)} %get-tuple-element.23.h, bf16[1,1024,1024]{2,1,0:T(8,128)(2,1)} %dy.1, bf16[1024,1024]{1,0:T(8,128)(2,1)} %get-tuple-element.24.first_a_t, bf16[2,1024,2816]{2,1,0:T(8,128)(2,1)} %w_gate.3, ...), custom_call_target="tpu_custom_call" | custom-call | tf_op jit(solution)/shard_map/backward_and_sum/pallas_call | solution.py:482
  278.5 41.0 %adamw.5 = (bf16[2,352,8,8,128]{4,3,2,1,0:T(8,128)(2,1)}, f32[2,352,8,8,128]{4,3,2,1,0:T(8,128)}, f32[2,352,8,8,128]{4,3,2,1,0:T(8,128)}) custom-call(bf16[2,352,8,8,128]{4,3,2,1,0:T(8,128)(2,1)} %bitcast.59, f32[2,352,8,8,128]{4,3,2,1,0:T(8,128)} %bitcast.62, f32[2,352,8,8,128]{4,3,2,1,0:T(8,128)} %bitcast.63, bf16[2,22,3,4,32,8,128]{6,5,4,3,2,1,0:T(8,128)(2,1)} %bitcast.56), custom_call_target="tpu_custom_call" | custom-call | tf_op jit(solution)/shard_map/adamw/pallas_call | solution.py:538
  319.5 41.1 %adamw.4 = (bf16[2,128,22,8,128]{4,3,2,1,0:T(8,128)(2,1)}, f32[2,128,22,8,128]{4,3,2,1,0:T(8,128)}, f32[2,128,22,8,128]{4,3,2,1,0:T(8,128)}) custom-call(bf16[2,128,22,8,128]{4,3,2,1,0:T(8,128)(2,1)} %bitcast.60, f32[2,128,22,8,128]{4,3,2,1,0:T(8,128)} %bitcast.64, f32[2,128,22,8,128]{4,3,2,1,0:T(8,128)} %bitcast.65, bf16[2,22,3,128,8,128]{5,4,3,2,1,0:T(8,128)(2,1)} %bitcast.57), custom_call_target="tpu_custom_call" | custom-call | tf_op jit(solution)/shard_map/adamw/pallas_call | solution.py:538
  360.6 41.1 %adamw.3 = (bf16[2,128,22,8,128]{4,3,2,1,0:T(8,128)(2,1)}, f32[2,128,22,8,128]{4,3,2,1,0:T(8,128)}, f32[2,128,22,8,128]{4,3,2,1,0:T(8,128)}) custom-call(bf16[2,128,22,8,128]{4,3,2,1,0:T(8,128)(2,1)} %bitcast.61, f32[2,128,22,8,128]{4,3,2,1,0:T(8,128)} %bitcast.66, f32[2,128,22,8,128]{4,3,2,1,0:T(8,128)} %bitcast.67, bf16[2,22,3,128,8,128]{5,4,3,2,1,0:T(8,128)(2,1)} %bitcast.58), custom_call_target="tpu_custom_call" | custom-call | tf_op jit(solution)/shard_map/adamw/pallas_call | solution.py:538

commit v4 on v3

--- a/solution.py
+++ b/solution.py
@@ -24,17 +24,24 @@
     _start += _n1 * SIZE[_axes[0]]
 assert _start == HALF
 FIN_SLOT, SWAP_SLOT, END_SLOT = 7, 15, 16
-HELD = 6
-PACE = 3
-LAST_CALLS, FIRST_CALLS = 4, 2
+SLOTS = 3
+HELD = 7
+PACE = 4
+LAST_CALLS, FIRST_CALLS = 3, 2
 COMPUTE_CALLS = BLOCKS * (LAST_CALLS + FIRST_CALLS)
 
 
 def ready(m):
-    return jnp.where(m < 5, 8 * m + 8, jnp.where(m == 5, 46, 4 * m + 26))
-
-
-CALLS = COMPUTE_CALLS + PACE * (END_SLOT + 1) + 1
+    return jnp.where(m < 5, 6 * m + 6, jnp.where(m == 5, 36, 4 * m + 16))
+
+
+LAST_TURN = PACE * (END_SLOT + 1)
+CALLS = COMPUTE_CALLS + LAST_TURN + 2
+
+
+def begun(call):
+    early = jnp.minimum(lax.div(jnp.maximum(call, 0), 6), 5)
+    return jnp.where(call < 36, early, jnp.minimum(lax.div(jnp.maximum(call - 12, 0), 4), UNITS))
 
 
 def ring_slots(n, hops):
@@ -108,8 +115,8 @@
         self.terms, self.out, self.own, self.par, self.r1, self.r2, self.r3, self.s3, self.fin = terms, out, own, par, r1, r2, r3, s3, fin
         self.send_rs, self.send_ag, self.recv, self.pair, self.load, self.written, self.credit = send_rs, send_ag, recv, pair, load, written, credit
         me = lax.axis_index("dp")
-        self.core = me % 2
-        self.place = {"x": me // 64, "y": me // 16 % 4, "z": me // 2 % 8}
+        self.core = lax.rem(me, 2)
+        self.place = {"x": lax.div(me, 64), "y": lax.rem(lax.div(me, 16), 4), "z": lax.rem(lax.div(me, 2), 8)}
         self.peers = [self.device()] + [self.device("x", d) for d in (1, 3)]
         self.peers += [self.device("y", d) for d in (1, 2, 3)] + [self.device("z", d) for d in range(1, 8)]
 
@@ -119,7 +126,7 @@
         if axis is None:
             core = 1 - core
         else:
-            at[axis] = (at[axis] + by + SIZE[axis]) % SIZE[axis]
+            at[axis] = lax.rem(at[axis] + (by + SIZE[axis]), SIZE[axis])
         return (0, ((at["x"] * 4 + at["y"]) * 8 + at["z"]) * 2 + core)
 
     def greet(self):
@@ -130,8 +137,8 @@
         pl.semaphore_wait(pltpu.get_barrier_semaphore(), len(self.peers))
 
     def begin(self, m):
-        for half in range(2):
-            arrived(self.out.at[0], HALF, self.written.at[half])
+        for block in range(2):
+            arrived(self.out.at[0], HALF, self.written.at[lax.rem(2 * m + block, SLOTS)])
 
         @pl.when(m >= HELD)
         def _():
@@ -139,15 +146,15 @@
             arrived(self.out.at[0], SENT, self.send_rs.at[m - HELD])
 
         unit = pl.ds(m * HALF, HALF)
-        pltpu.make_async_copy(self.terms.at[self.core, unit], self.own.at[m % HELD], self.load.at[m, 0]).start()
-        remote(self.terms.at[1 - self.core, unit], self.par.at[m % HELD], self.send_rs.at[m], self.pair.at[m, 0], self.device()).start()
+        pltpu.make_async_copy(self.terms.at[self.core, unit], self.own.at[lax.rem(m, HELD)], self.load.at[m, 0]).start()
+        remote(self.terms.at[1 - self.core, unit], self.par.at[lax.rem(m, HELD)], self.send_rs.at[m], self.pair.at[m, 0], self.device()).start()
 
     def color_stage(self, c, stage, m):
         axes, start, (n1, n2, n3), _ = COLORS[c]
         k1, k2, k3 = (SIZE[a] for a in axes)
         p1, p2, p3 = (self.place[a] for a in axes)
         h1, h2 = k1 // 2, k2 // 2
-        b = m % HELD
+        b = lax.rem(m, HELD)
         o, q, a1, a2, a3 = (ref.at[b] for ref in (self.own, self.par, self.r1, self.r2, self.r3))
         result, mine = self.out.at[self.core], m * HALF
         send_rs, send_ag, load = self.send_rs.at[m], self.send_ag.at[m], self.load.at[m, 1 + c]
@@ -163,7 +170,7 @@
             h = k // 2
             j = h - hop
             for way, sign in ((0, 1), (1, -1)):
-                owner = (p + sign * j + k) % k
+                owner = lax.rem(p + (sign * j + k), k)
                 at = base + owner * n
                 lo, size = (0, n) if j < h else ((0, n - n // 2) if way == 0 else (n - n // 2, n // 2))
                 extra = [(ref, where + owner * n) for ref, where in more]
@@ -199,7 +206,7 @@
                 gather_wait(k, n, hop - 1, kind)
             for way, sign in ((0, 1), (1, -1)):
                 lo, size = gather_sizes(k, n, hop)[way]
-                piece = result.at[pl.ds(mine + base + (p - sign * hop + k) % k * n + lo, size)]
+                piece = result.at[pl.ds(mine + base + lax.rem(p + (k - sign * hop), k) * n + lo, size)]
                 remote(piece, piece, send_ag, sem(kind, 2 * hop + way), device(axis, sign)).start()
 
         last1 = [(a1, LAY.r1[c][h1 - 1][way][0]) for way in range(2)]
@@ -218,7 +225,7 @@
             ring_wait(h2, LAY.r2[c], a2, "r2")
             add_tiles(self.s3.at[b], LAY.s3[c], n2, [(o, base3), (q, base3)] + [(r, w + p2 * n2) for r, w in last1] + last2)
             for d in range(1, k3):
-                piece = self.s3.at[b, pl.ds(LAY.s3[c] + (p3 + d) % k3 * n3, n3)]
+                piece = self.s3.at[b, pl.ds(LAY.s3[c] + lax.rem(p3 + d, k3) * n3, n3)]
                 remote(piece, a3.at[pl.ds(LAY.r3[c] + (d - 1) * n3, n3)], send_rs, sem("r3"), device(axes[2], d)).start()
             return
         stage -= 1
@@ -275,19 +282,19 @@
         def unit(m, _):
             since = call - ready(m)
 
-            @pl.when((since >= 0) & (since <= PACE * (END_SLOT + 1)) & (since % PACE == 0))
+            @pl.when(lax.rem(since, PACE) == 0)
             def _():
-                s = since // PACE - 1
-                for low in range(-1, END_SLOT + 1, 3):
-
-                    @pl.when((s >= low) & (s < low + 3))
+                s = lax.div(since, PACE) - 1
+                for low in range(-1, END_SLOT + 1, 4):
+
+                    @pl.when((s >= low) & (s < low + 4))
                     def _():
-                        for one in range(low, min(low + 3, END_SLOT + 1)):
+                        for one in range(low, min(low + 4, END_SLOT + 1)):
                             pl.when(s == one)(lambda one=one: self.slot(one, m))
 
             return 0
 
-        lax.fori_loop(0, UNITS, unit, 0)
+        lax.fori_loop(begun(call - LAST_TURN - 1), begun(call), unit, 0)
 
     def finish(self):
         def unit(m, _):
@@ -324,21 +331,16 @@
     def _():
         norm_rows(h, a)
         a_t[...] = a[...].T
+        total[...] = jnp.zeros_like(total)
 
     gate = dot(a[...], w_gate[0])
     up = dot(a[...], w_up[0])
     gate_out[...] = gate
     up_out[...] = up
     hidden = (gate * jax.nn.sigmoid(gate) * up).astype(BF16)
-    part = dot(hidden, w_down[0])
-
-    @pl.when(step == 0)
-    def _():
-        total[...] = part
-
-    @pl.when(step > 0)
-    def _():
-        total[...] += part
+    for i in range(4):
+        columns = slice(i * 256, (i + 1) * 256)
+        total[:, columns] += dot(hidden, w_down[0, :, columns])
 
     @pl.when(step == pl.num_programs(0) - 1)
     def _():
@@ -359,12 +361,13 @@
 
 
 def backward_kernel(h, dy, first_a_t, w_gate, w_up, w_down, first_gate, first_up, out, terms, *scratch):
-    a, a_t, total, by_h, gate, up, hidden, by_gate, by_up, grads, *held = scratch
+    a, a_t, total, hidden, by_gate, by_up, grads, *held = scratch
+    by_h = a
     engine = Engine(terms, out, *held)
     written = engine.written
     step = pl.program_id(0)
     last, first = step < BLOCKS, (step >= BLOCKS) & (step < 2 * BLOCKS)
-    slot = step % 2
+    slot = lax.rem(step, SLOTS)
 
     @pl.when(step == 0)
     def _():
@@ -400,26 +403,22 @@
 
         @pl.when(last & (k == 0))
         def _():
-            gate[...] = dot(a[...], w_gate[0])
-            up[...] = dot(a[...], w_up[0])
+            gate, up = dot(a[...], w_gate[0]), dot(a[...], w_up[0])
+            hidden[...], by_gate[...], by_up[...] = hidden_backward(gate, up, dot(dy[0], w_down[0], (1, 1)))
+            by_down(dy[0])
 
         @pl.when(last & (k == 1))
         def _():
-            hidden[...], by_gate[...], by_up[...] = hidden_backward(gate[...], up[...], dot(dy[0], w_down[0], (1, 1)))
-            by_down(dy[0])
+            by_wide(a_t[...])
 
         @pl.when(last & (k == 2))
-        def _():
-            by_wide(a_t[...])
-
-        @pl.when(last & (k == 3))
         def _():
             for i in range(4):
                 columns = pl.ds(i * 256, 256)
                 value = dot(by_gate[...], w_gate[0, columns, :], (1, 1)) + dot(by_up[...], w_up[0, columns, :], (1, 1))
                 total[:, columns] = jnp.where(step == 0, value, total[:, columns] + value)
 
-        @pl.when((step == BLOCKS - 1) & (k == 3))
+        @pl.when((step == BLOCKS - 1) & (k == 2))
         def _():
             def some(rows):
                 wide = h[0, rows, :].astype(F32)
@@ -486,11 +485,10 @@
         in_specs=[whole, whole, turned, wide, wide, tall, hidden, hidden],
         out_specs=[pl.BlockSpec(memory_space=pl.ANY)] * 2,
         scratch_shapes=[
-            vmem(tokens, d), vmem(d, tokens), vmem(tokens, d, dtype=F32), vmem(tokens, d),
-            vmem(tokens, BLOCK, dtype=F32), vmem(tokens, BLOCK, dtype=F32), vmem(tokens, BLOCK), vmem(tokens, BLOCK), vmem(tokens, BLOCK),
-            tiles(2, 3, 256),
+            vmem(tokens, d), vmem(d, tokens), vmem(tokens, d, dtype=F32),
+            vmem(tokens, BLOCK), vmem(tokens, BLOCK), vmem(tokens, BLOCK), tiles(SLOTS, 3, 256),
             tiles(HELD, HALF), tiles(HELD, HALF), tiles(HELD, LAY.n1), tiles(HELD, LAY.n2), tiles(HELD, LAY.n3), tiles(HELD, LAY.ns), tiles(UNITS, LAY.nf),
-            dma((UNITS,)), dma((UNITS,)), dma((UNITS, LAY.sems)), dma((UNITS, 2)), dma((UNITS, 4)), dma((2,)),
+            dma((UNITS,)), dma((UNITS,)), dma((UNITS, LAY.sems)), dma((UNITS, 2)), dma((UNITS, 4)), dma((SLOTS,)),
             pltpu.SemaphoreType.REGULAR((UNITS - HELD,)),
         ],
         compiler_params=pltpu.CompilerParams(collective_id=0, has_side_effects=True, vmem_limit_bytes=67043328),

time: 402 us -> 390 us (0.970)
  Pallas kernels: 401 us -> 389 us
    pallas_call x1, Pallas kernels: 246 us -> 237 us  [summed_gradients(): pl.pallas_call(backward_kernel, out_shape=[total, total], grid=(2 * BLOCK...]
where the time goes in v4:
time: 390 us
  Pallas kernels  389 us (100%)
    pallas_call x1, Pallas kernels, summed_gradients(): pl.pallas_call(backward_kernel, out_shape=[total, total], grid=(2 * BLOCK...  237 us
    pallas_call x3, Pallas kernels, adamw(): pl.pallas_call(kernel, out_shape=[jax.ShapeDtypeStruct(a.shape, a.dtype)...  123 us
    pallas_call x1, Pallas kernels, summed_gradients(): pl.pallas_call(forward_kernel, out_shape=[jax.ShapeDtypeStruct((tokens, f...  29.2 us

profile of v4, /device:TPU:1, one launch (start us, length us, event | category | flops | bytes accessed | tf_op | source)
XLA Modules:
  0.0 390.0 jit_solution(2658211601007593319)
XLA Ops:
  0.6 29.2 %first_layer_forward.1 = (f32[1024,2816]{1,0:T(8,128)}, f32[1024,2816]{1,0:T(8,128)}, bf16[1,1024,1024]{2,1,0:T(8,128)(2,1)}, bf16[1024,1024]{1,0:T(8,128)(2,1)}) custom-call(bf16[1,1024,1024]{2,1,0:T(8,128)(2,1)} %h.1, bf16[2,1024,2816]{2,1,0:T(8,128)(2,1)} %w_gate.3, bf16[2,1024,2816]{2,1,0:T(8,128)(2,1)} %w_up.3, bf16[2,2816,1024]{2,1,0:T(8,128)(2,1)} %w_down.3), custom_call_target="tpu_custom_call" | custom-call | tf_op jit(solution)/shard_map/first_layer_forward/pallas_call | solution.py:463
  29.9 236.9 %backward_and_sum.1 = (bf16[2,8448,8,128]{3,2,1,0:T(8,128)(2,1)}, bf16[2,8448,8,128]{3,2,1,0:T(8,128)(2,1)}) custom-call(bf16[1,1024,1024]{2,1,0:T(8,128)(2,1)} %get-tuple-element.23.h, bf16[1,1024,1024]{2,1,0:T(8,128)(2,1)} %dy.1, bf16[1024,1024]{1,0:T(8,128)(2,1)} %get-tuple-element.24.first_a_t, bf16[2,1024,2816]{2,1,0:T(8,128)(2,1)} %w_gate.3, ...), custom_call_target="tpu_custom_call" | custom-call | tf_op jit(solution)/shard_map/backward_and_sum/pallas_call | solution.py:481
  266.8 41.0 %adamw.5 = (bf16[2,352,8,8,128]{4,3,2,1,0:T(8,128)(2,1)}, f32[2,352,8,8,128]{4,3,2,1,0:T(8,128)}, f32[2,352,8,8,128]{4,3,2,1,0:T(8,128)}) custom-call(bf16[2,352,8,8,128]{4,3,2,1,0:T(8,128)(2,1)} %bitcast.59, f32[2,352,8,8,128]{4,3,2,1,0:T(8,128)} %bitcast.62, f32[2,352,8,8,128]{4,3,2,1,0:T(8,128)} %bitcast.63, bf16[2,22,3,4,32,8,128]{6,5,4,3,2,1,0:T(8,128)(2,1)} %bitcast.56), custom_call_target="tpu_custom_call" | custom-call | tf_op jit(solution)/shard_map/adamw/pallas_call | solution.py:536
  307.8 41.1 %adamw.4 = (bf16[2,128,22,8,128]{4,3,2,1,0:T(8,128)(2,1)}, f32[2,128,22,8,128]{4,3,2,1,0:T(8,128)}, f32[2,128,22,8,128]{4,3,2,1,0:T(8,128)}) custom-call(bf16[2,128,22,8,128]{4,3,2,1,0:T(8,128)(2,1)} %bitcast.60, f32[2,128,22,8,128]{4,3,2,1,0:T(8,128)} %bitcast.64, f32[2,128,22,8,128]{4,3,2,1,0:T(8,128)} %bitcast.65, bf16[2,22,3,128,8,128]{5,4,3,2,1,0:T(8,128)(2,1)} %bitcast.57), custom_call_target="tpu_custom_call" | custom-call | tf_op jit(solution)/shard_map/adamw/pallas_call | solution.py:536
  348.9 41.1 %adamw.3 = (bf16[2,128,22,8,128]{4,3,2,1,0:T(8,128)(2,1)}, f32[2,128,22,8,128]{4,3,2,1,0:T(8,128)}, f32[2,128,22,8,128]{4,3,2,1,0:T(8,128)}) custom-call(bf16[2,128,22,8,128]{4,3,2,1,0:T(8,128)(2,1)} %bitcast.61, f32[2,128,22,8,128]{4,3,2,1,0:T(8,128)} %bitcast.66, f32[2,128,22,8,128]{4,3,2,1,0:T(8,128)} %bitcast.67, bf16[2,22,3,128,8,128]{5,4,3,2,1,0:T(8,128)(2,1)} %bitcast.58), custom_call_target="tpu_custom_call" | custom-call | tf_op jit(solution)/shard_map/adamw/pallas_call | solution.py:536
